TPU v7x, 128 devices: a whole 4x4x4 slice. The times are simulated.
128 devices in a mesh: pages: 16 (over y, x_hi, core), heads: 8 (over x_lo, z).
Axes of the slice: x: 4 (x_hi: 2, x_lo: 2; x = x_hi * 2 + x_lo), y: 4, z: 4, core: 2. Of those that a mesh axis runs over, the one named last changes fastest.
Arguments:
- queries: bfloat16 [1024, 32, 128], P('pages', 'heads'), may hold values from -6 to 6
- keys: bfloat16 [1152, 16, 128, 128], P('pages', 'heads'), may hold values from -6 to 6
- values: bfloat16 [1152, 16, 128, 128], P('pages', 'heads'), may hold values from -6 to 6
- hot_pages: int32 [64], replicated, may hold values from 0 to 1151, as said below
- hot_used: int32 [1024], replicated, may hold values from 1 to 64
- user_pages: int32 [1024, 1], P('pages'), may hold values from 8 to 71, as said below
- lengths: int32 [1024], P('pages'), may hold values from 1 to 128
- o_weight: bfloat16 [4096, 4608], P('heads'), may hold values from -0.09375 to 0.09375
- residual: bfloat16 [1024, 4608], P(('pages', 'heads')), may hold values from -6 to 6
- norm_gain: float32 [4608], replicated, may hold values from 0.25 to 1.75
Outputs:
- output: bfloat16 [1024, 4608], P(('pages', 'heads'))
Inputs may be any that keep to these rules, and one draw needn't show every extreme that they name: `hot_pages`: 64 distinct pages; each lies among the first 8 pages of its group (page p belongs to group p // 72); one group holds exactly 8 of them and none holds more. `user_pages`: numbers within the sequence's own group (sequence s belongs to group s // 64); all own pages of the sequences of one group are distinct.
All inputs are finite; a program needn't handle non-finite values.
Results may differ from a plain program's by a relative error of at most 0.019.
Values may be sent and summed in bfloat16 or wider, within the bound.
A program may use at most 128 MiB of HBM per device.

v0:
```python
import math

import jax
import jax.numpy as jnp
from jax import lax
from jax.sharding import PartitionSpec as P

HOT_CAP = 8


score_scale = 1.0 / 12.0
soft_cap = 50.0
epsilon = 1e-06


def from_everyone(shard, axis):
    copies = jnp.broadcast_to(shard, (lax.axis_size(axis), *shard.shape))
    return lax.all_to_all(copies, axis, split_axis=0, concat_axis=0, tiled=True)


def joined_along(parts, dim):
    shape = list(parts.shape[1:])
    shape[dim] *= parts.shape[0]
    return jnp.moveaxis(parts, 0, dim).reshape(shape)


def gather_directly(shard, axis, dim):
    parts = from_everyone(shard, axis)
    return joined_along(parts, dim)


def split_up(shard, dim, count):
    shape = shard.shape
    parts = shard.reshape(*shape[:dim], count, shape[dim] // count, *shape[dim + 1 :])
    return jnp.moveaxis(parts, dim, 0)


def sent_and_summed(shard, axis, dim):
    count = lax.axis_size(axis)
    parts = lax.all_to_all(split_up(shard, dim, count), axis, 0, 0, tiled=True)
    return jnp.sum(parts.astype(jnp.float32), axis=0)


def sent_together(arrays, axis, dim, along):
    widths = [math.prod(a.shape[along:]) for a in arrays]
    both = jnp.concatenate(
        [a.reshape(*a.shape[:along], w) for a, w in zip(arrays, widths)], axis=along
    )
    whole = sent_and_summed(both, axis, dim)
    parts = jnp.split(whole, [sum(widths[:k]) for k in range(1, len(widths))], axis=along)
    return tuple((b.reshape(*whole.shape[:along], *a.shape[along:]) for a, b in zip(arrays, parts)))


def shared_terms(grouped, page_keys, page_values, allowed):
    logits = jnp.einsum("skgd,pktd->skgpt", grouped, page_keys, preferred_element_type=jnp.float32)
    weight = jnp.exp(soft_cap * jnp.tanh(logits * (score_scale / soft_cap)))
    weight = jnp.where(allowed[:, None, None, :, None], weight, 0.0)
    numerator = jnp.einsum(
        "skgpt,pktd->skgd",
        weight.astype(jnp.bfloat16),
        page_values,
        preferred_element_type=jnp.float32,
    )
    return (numerator, jnp.sum(weight, axis=(3, 4)))


def own_terms(grouped, owned_keys, owned_values, lengths):
    logits = jnp.einsum(
        "skgd,suktd->skgut", grouped, owned_keys, preferred_element_type=jnp.float32
    )
    page_len = owned_keys.shape[3]
    token_pos = (
        jnp.arange(owned_keys.shape[1], dtype=jnp.int32)[:, None] * page_len
        + jnp.arange(page_len, dtype=jnp.int32)[None, :]
    )
    allowed = token_pos[None, :, :] < lengths[:, None, None]
    weight = jnp.exp(soft_cap * jnp.tanh(logits * (score_scale / soft_cap)))
    weight = jnp.where(allowed[:, None, None, :, :], weight, 0.0)
    numerator = jnp.einsum(
        "skgut,suktd->skgd",
        weight.astype(jnp.bfloat16),
        owned_values,
        preferred_element_type=jnp.float32,
    )
    return (numerator, jnp.sum(weight, axis=(3, 4)))


def slot_places(page_ids, hot_pages):
    hot_order = jnp.arange(hot_pages.shape[0], dtype=jnp.int32)
    matches = page_ids[:, None] == hot_pages[None, :]
    present = jnp.any(matches, axis=1)
    position = jnp.sum(jnp.where(matches, hot_order[None, :], 0), axis=1)
    return (present, position)


def per_device(
    queries, keys, values, hot_pages, hot_used, user_pages, lengths, o_weight, residual, norm_gain
):
    seq_dev, head_count, head_dim = queries.shape
    kv_heads = keys.shape[1]
    group_size = head_count // kv_heads
    page_count = keys.shape[0]
    grouped = queries.reshape(seq_dev, kv_heads, group_size, head_dim)
    myself = lax.axis_index("pages")
    hot_keys = keys[:HOT_CAP]
    hot_values = values[:HOT_CAP]
    everyone = gather_directly(queries, "pages", 0)
    page_ids = myself * page_count + jnp.arange(HOT_CAP, dtype=jnp.int32)
    present, position = slot_places(page_ids, hot_pages)
    allowed = present[None, :] & (position[None, :] < hot_used[:, None])
    everyone_grouped = everyone.reshape(everyone.shape[0], kv_heads, group_size, head_dim)
    numerator, totals = shared_terms(everyone_grouped, hot_keys, hot_values, allowed)
    numerator, totals = sent_together(
        (numerator.astype(jnp.bfloat16), totals.astype(jnp.bfloat16)), "pages", 0, 3
    )
    owned_keys = keys[user_pages]
    owned_values = values[user_pages]
    own_numerator, own_totals = own_terms(grouped, owned_keys, owned_values, lengths)
    attended = ((numerator + own_numerator) / (totals + own_totals)[:, :, :, None]).astype(
        jnp.bfloat16
    )
    attended = attended.reshape(seq_dev, head_count * head_dim)
    projected = sent_and_summed(
        jnp.dot(attended, o_weight, preferred_element_type=jnp.float32).astype(jnp.bfloat16),
        "heads",
        0,
    )
    mean_sq = jnp.mean(projected * projected, axis=1, keepdims=True)
    normed = projected / jnp.sqrt(mean_sq + epsilon) * norm_gain[None, :]
    return (residual.astype(jnp.float32) + normed).astype(jnp.bfloat16)


def solution(mesh):
    in_specs = (
        P("pages", "heads", None),
        P("pages", "heads", None, None),
        P("pages", "heads", None, None),
        P(),
        P(),
        P("pages", None),
        P("pages"),
        P("heads", None),
        P(("pages", "heads"), None),
        P(),
    )
    out_specs = P(("pages", "heads"), None)
    return jax.shard_map(
        per_device, mesh=mesh, in_specs=in_specs, out_specs=out_specs, check_vma=False
    )
```

profile of v0, /device:TPU:0, one launch (start us, length us, event | category | flops | bytes accessed | tf_op | source)
XLA Modules:
  0.0 106.3 jit_solution(14115427346754082940)
XLA Ops:
  0.0 0.8 copy.36
  0.9 1.2 %broadcast_in_dim.58 = bf16[16,64,4,128]{3,1,2,0:T(8,128)(2,1)} broadcast(bf16[64,4,128]{2,0,1:T(8,128)(2,1)S(1)} %copy.36), dimensions={1,2,3} | broadcast | bytes 1114112 | tf_op jit(solution)/shard_map/broadcast_in_dim | solution.py:17
  2.1 7.1 %all-to-all-start = ((bf16[16,64,4,128]{3,1,2,0:T(8,128)(2,1)}), bf16[16,64,4,128]{3,1,2,0:T(8,128)(2,1)S(1)}, u32[]{:S(2)}, u32[]{:S(2)}) async-start(bf16[16,64,4,128]{3,1,2,0:T(8,128)(2,1)} %broadcast_in_dim.58), calls=%async_computation | async-start | bytes 2097152 | tf_op jit(solution)/shard_map/all_to_all | solution.py:18
  9.3 0.8 compare_reduce_fusion
  10.1 0.8 fusion.19
  10.9 0.8 compare_and_fusion
  11.7 15.5 %all-to-all-done = bf16[16,64,4,128]{3,1,2,0:T(8,128)(2,1)S(1)} async-done(((bf16[16,64,4,128]{3,1,2,0:T(8,128)(2,1)}), bf16[16,64,4,128]{3,1,2,0:T(8,128)(2,1)S(1)}, u32[]{:S(2)}, u32[]{:S(2)}) %all-to-all-start) | async-done | bytes 1048608 | tf_op jit(solution)/shard_map/all_to_all | solution.py:18
  27.2 0.1 copy.37
  27.3 9.2 %fusion = (bf16[1024,2,2]{0,2,1:T(2,128)(2,1)S(1)}, f32[2,8,128,1024,2]{3,2,4,1,0:T(8,128)}) fusion(pred[1024,8]{0,1:T(8,128)(4,1)S(1)} %compare_and_fusion, bf16[1024,2,2,128,1]{3,0,2,4,1:T(8,128)(2,1)S(1)} %bitcast.54, bf16[72,2,128,128]{3,2,1,0:T(8,128)(2,1)} %param.11), kind=kOutput, calls=%fused_computation.3 | convolution fusion | flops 1090514944 | bytes 18366464 | tf_op jit(solution)/shard_map/skgd,pktd->skgpt/dot_general | solution.py:55
  36.6 0.1 convert_element_type.50
  36.7 0.5 copy.41
  37.2 9.2 %bitcast_convert_fusion = bf16[2,1024,2,128]{3,1,2,0:T(8,128)(2,1)S(1)} fusion(f32[2,8,128,1024,2]{3,2,4,1,0:T(8,128)} %get-tuple-element.6, pred[1024,8]{0,1:T(8,128)(4,1)S(1)} %compare_and_fusion, bf16[72,2,128,128]{3,2,1,0:T(8,128)(2,1)} %param.12), kind=kOutput, calls=%fused_computation.10 | convolution fusion | flops 1091043328 | bytes 18358272 | tf_op jit(solution)/shard_map/skgpt,pktd->skgd/dot_general | solution.py:58
  46.4 0.0 copy-start.4
  46.4 2.1 %pad_maximum_fusion = bf16[16,64,2,2,129]{4,1,3,2,0:T(8,128)(2,1)} fusion(bf16[16,64,2,2,1]{4,1,3,2,0:T(8,128)(2,1)S(1)} %copy.41, bf16[16,64,2,2,128]{4,1,0,3,2:T(8,128)(2,1)S(1)} %bitcast.55), kind=kLoop, calls=%fused_computation.11 | loop fusion | flops 2113536 | bytes 2113536 | tf_op jit(solution)/shard_map/concatenate | solution.py:46
  48.4 3.9 %all-to-all-start.1 = ((bf16[16,64,2,2,129]{4,1,3,2,0:T(8,128)(2,1)}), bf16[16,64,2,2,129]{4,1,3,2,0:T(8,128)(2,1)S(1)}, u32[]{:S(2)}, u32[]{:S(2)}) async-start(bf16[16,64,2,2,129]{4,1,3,2,0:T(8,128)(2,1)} %pad_maximum_fusion), calls=%async_computation.1 | async-start | bytes 4194304 | tf_op jit(solution)/shard_map/all_to_all | solution.py:40
  52.3 0.0 copy-done.4
  52.4 5.4 %gather_fusion = bf16[64,2,128,128]{3,2,1,0:T(8,128)(2,1)} fusion(bf16[72,2,128,128]{3,2,1,0:T(8,128)(2,1)} %param.11, s32[1024]{0:T(1024)S(1)} %pad_clamp_fusion), kind=kCustom, calls=%fused_computation | custom fusion | bytes 8388864 | tf_op jit(solution)/shard_map/gather | solution.py:116
  57.8 0.0 copy-start.3
  57.8 0.0 copy-start.1
  57.8 5.4 %gather_fusion.1 = bf16[64,2,128,128]{3,2,1,0:T(8,128)(2,1)} fusion(bf16[72,2,128,128]{3,2,1,0:T(8,128)(2,1)} %param.12, s32[1024]{0:T(1024)S(1)} %pad_clamp_fusion), kind=kCustom, calls=%fused_computation.1 | custom fusion | bytes 8388864 | tf_op jit(solution)/shard_map/gather | solution.py:117
  63.2 0.0 copy-done.3
  63.2 0.1 iota_compare_fusion
  63.2 0.0 copy-done.1
  63.2 4.6 %fusion.24 = (f32[64,2,2]{2,1,0:T(2,128)S(1)}, bf16[64,2,2,128]{3,2,1,0:T(2,128)(2,1)S(1)}) fusion(bf16[64,2,128,128]{3,2,1,0:T(8,128)(2,1)} %gather_fusion, bf16[64,2,2,128]{3,2,1,0:T(2,128)(2,1)S(1)} %bitcast.58, pred[64,128]{1,0:T(8,128)(4,1)S(1)} %iota_compare_fusion), kind=kOutput, calls=%fused_computation.43 | convolution fusion | flops 8552192 | bytes 4334592 | tf_op jit(solution)/shard_map/skgd,suktd->skgut/dot_general | solution.py:68
  67.8 0.9 copy.45
  68.8 12.6 %all-to-all-done.1 = bf16[16,64,2,2,129]{4,1,3,2,0:T(8,128)(2,1)S(1)} async-done(((bf16[16,64,2,2,129]{4,1,3,2,0:T(8,128)(2,1)}), bf16[16,64,2,2,129]{4,1,3,2,0:T(8,128)(2,1)S(1)}, u32[]{:S(2)}, u32[]{:S(2)}) %all-to-all-start.1) | async-done | bytes 1056800 | tf_op jit(solution)/shard_map/all_to_all | solution.py:40
  81.4 0.4 convert_reduce_fusion
  81.8 0.9 copy.55
  82.7 3.4 %fusion.14 = bf16[64,2,2,128]{3,2,1,0:T(2,128)(2,1)S(1)} fusion(bf16[64,2,128,128]{3,2,1,0:T(8,128)(2,1)} %gather_fusion.1, f32[64,2,2,128]{3,0,2,1:T(8,128)S(1)} %split.8, f32[64,2,2]{2,1,0:T(2,128)S(1)} %bitcast.56, bf16[64,2,2,128]{3,2,1,0:T(2,128)(2,1)S(1)} %get-tuple-element.8), kind=kOutput, calls=%fused_computation.21 | convolution fusion | flops 8486912 | bytes 4457472 | tf_op jit(solution)/shard_map/skgut,suktd->skgd/dot_general | solution.py:79
  86.1 0.0 copy-start
  86.1 0.0 copy-start.2
  86.2 3.3 %fusion.5 = bf16[8,8,4608]{2,1,0:T(8,128)(2,1)S(1)} fusion(bf16[64,512]{1,0:T(8,128)(2,1)S(1)} %reshape.120, bf16[512,4608]{1,0:T(8,128)(2,1)} %param.17), kind=kOutput, calls=%fused_computation.8 | convolution fusion | flops 302284800 | bytes 5373952 | tf_op jit(solution)/shard_map/dot_general | solution.py:124
  89.4 15.9 %all_to_all.15 = bf16[8,8,4608]{2,1,0:T(8,128)(2,1)S(1)} all-to-all(bf16[8,8,4608]{2,1,0:T(8,128)(2,1)S(1)} %fusion.5), channel_id=1, replica_groups=mesh['pages'=16,'heads'=8] {'heads'}, dimensions={0} | all-to-all | bytes 1179648 | tf_op jit(solution)/shard_map/all_to_all | solution.py:40
  105.3 0.1 convert_reduce_fusion.1
  105.4 0.2 multiply_reduce_fusion
  105.6 0.0 copy-done
  105.6 0.0 copy-done.2
  105.6 0.7 add_convert_fusion
  (7 shorter events, 0.1 us)
Async XLA Ops:
  2.1 25.1 %all-to-all-start = ((bf16[16,64,4,128]{3,1,2,0:T(8,128)(2,1)}), bf16[16,64,4,128]{3,1,2,0:T(8,128)(2,1)S(1)}, u32[]{:S(2)}, u32[]{:S(2)}) async-start(bf16[16,64,4,128]{3,1,2,0:T(8,128)(2,1)} %broadcast_in_dim.58), calls=%async_computation | async-start | bytes 2097152 | tf_op jit(solution)/shard_map/all_to_all | solution.py:18
  46.4 6.0 %copy-start.4 = (s32[64,1]{0,1:T(1,128)S(1)}, s32[64,1]{0,1:T(1,128)}, u32[]{:S(2)}) copy-start(s32[64,1]{0,1:T(1,128)} %param.15) | copy-start | bytes 772
  48.4 33.0 %all-to-all-start.1 = ((bf16[16,64,2,2,129]{4,1,3,2,0:T(8,128)(2,1)}), bf16[16,64,2,2,129]{4,1,3,2,0:T(8,128)(2,1)S(1)}, u32[]{:S(2)}, u32[]{:S(2)}) async-start(bf16[16,64,2,2,129]{4,1,3,2,0:T(8,128)(2,1)} %pad_maximum_fusion), calls=%async_computation.1 | async-start | bytes 4194304 | tf_op jit(solution)/shard_map/all_to_all | solution.py:40
  57.8 5.4 %copy-start.3 = (s32[64]{0:T(128)S(1)}, s32[64]{0:T(128)}, u32[]{:S(2)}) copy-start(s32[64]{0:T(128)} %param.16) | copy-start | bytes 772
  57.8 5.5 %copy-start.1 = (bf16[64,4,128]{2,1,0:T(4,128)(2,1)S(1)}, bf16[64,4,128]{2,1,0:T(4,128)(2,1)}, u32[]{:S(2)}) copy-start(bf16[64,4,128]{2,1,0:T(4,128)(2,1)} %param.10) | copy-start | bytes 196612
  86.1 19.5 %copy-start = (bf16[8,4608]{1,0:T(8,128)(2,1)S(1)}, bf16[8,4608]{1,0:T(8,128)(2,1)}, u32[]{:S(2)}) copy-start(bf16[8,4608]{1,0:T(8,128)(2,1)} %param.18) | copy-start | bytes 221188
  86.1 19.5 %copy-start.2 = (f32[4608]{0:T(1024)S(1)}, f32[4608]{0:T(1024)}, u32[]{:S(2)}) copy-start(f32[4608]{0:T(1024)} %param.19) | copy-start | bytes 55300
where the time goes:
time: 107 us; the launch traced here: 106 us
  matrix products  29.6 us (28%)
  waiting for transfers between devices  28.2 us (26%)
  blocking collectives  15.9 us (15%)
  local copies, waits for them, and re-layouts  15.5 us (14%)
  starting transfers between devices  11 us (10%)
  other arithmetic  5.97 us (6%)
    all_to_all x1, blocking collectives, sent_and_summed(): parts = lax.all_to_all(split_up(shard, dim, count), axis, 0, 0, tiled=True)  15.9 us
    all_to_all x1, waiting for transfers between devices, from_everyone(): return lax.all_to_all(copies, axis, split_axis=0, concat_axis=0, tiled=True)  15.5 us
    all_to_all x1, waiting for transfers between devices, sent_and_summed(): parts = lax.all_to_all(split_up(shard, dim, count), axis, 0, 0, tiled=True)  12.6 us
    dot_general x1, matrix products, shared_terms(): jnp.einsum('skgd,pktd->skgpt', grouped, page_keys, preferred_element_type...  9.23 us
    dot_general x1, matrix products, shared_terms(): jnp.einsum('skgpt,pktd->skgd', weight.astype(jnp.bfloat16), page_values,...  9.16 us
    all_to_all x1, starting transfers between devices, from_everyone(): return lax.all_to_all(copies, axis, split_axis=0, concat_axis=0, tiled=True)  7.15 us
    gather x1, local copies, waits for them, and re-layouts, per_device(): owned_keys = keys[user_pages]  5.39 us
    gather x1, local copies, waits for them, and re-layouts, per_device(): owned_values = values[user_pages]  5.38 us
  transfers between devices with their start and end apart: 2, of which 2 were waited for; matrix products, arithmetic and copies ran while one was open for 18% of the time, Pallas kernels for 0%

commit v1 on v0

v1 whole, which is shorter than its diff:
```python
import functools
import math

import jax
import jax.numpy as jnp
from jax import lax
from jax.experimental import pallas as pl
from jax.experimental.pallas import tpu as pltpu
from jax.sharding import PartitionSpec as P

HOT_CAP = 8
soft_cap = 50.0
score_scale = 1.0 / 12.0
epsilon = 1e-06
NY = 4
F32, BF16, I32 = jnp.float32, jnp.bfloat16, jnp.int32
MESH = pl.DeviceIdType.MESH

A0, A3, A1, A2, B3, B1, B2, B0 = range(8)
OWNER = {A0: (0, 0), A3: (3, 0), A1: (1, 0), A2: (2, 0), B3: (3, 1), B1: (1, 1), B2: (2, 1), B0: (0, 1)}


def weights_of(logits):
    return jnp.exp2(jnp.tanh(logits * (score_scale / soft_cap)) * (soft_cap * math.log2(math.e)))


def split_sum(totals, rows):
    high = totals.astype(BF16).astype(F32)
    row = lax.broadcasted_iota(I32, (16, rows), 0)
    return jnp.where(row == 0, high, jnp.where(row == 1, totals - high, 0.0)).astype(BF16)


def attention_kernel(
    q_hbm, k_hbm, v_hbm, hot_hbm, used_hbm, up_hbm, len_hbm, out_ref,
    q_v, hot_v, used_v, len_v, up_s, kbuf, vbuf, hk, hv, vt, qt, qbd, wt, urow, lrow, pos,
    res, ra, rb, rx, bsum, own_t, own_w, own_o,
    in_sem, kv_send, kv_recv, ag_send, ag_recv, rs_send, rs_recv,
):
    seqs = len_v.shape[1]
    kvh, page, hd = hk.shape[1:]
    rows = q_v.shape[0]
    half = rows // kvh
    me = lax.axis_index("pages")
    y, xh, core = me // 4, (me // 2) % 2, me % 2

    def at(dy, dx=0, dc=0):
        return {"pages": ((y + dy) % NY) * 4 + ((xh + dx) % 2) * 2 + (core + dc) % 2}

    def remote(src, dst, send, recv, target):
        return pltpu.make_async_remote_copy(
            src_ref=src, dst_ref=dst, send_sem=send, recv_sem=recv, device_id=target, device_id_type=MESH
        )

    local = [
        pltpu.make_async_copy(q_hbm, q_v, in_sem.at[0]),
        pltpu.make_async_copy(hot_hbm, hot_v, in_sem.at[1]),
        pltpu.make_async_copy(used_hbm, used_v, in_sem.at[2]),
        pltpu.make_async_copy(len_hbm, len_v, in_sem.at[3]),
        pltpu.make_async_copy(up_hbm, up_s, in_sem.at[4]),
        pltpu.make_async_copy(v_hbm.at[pl.ds(0, HOT_CAP)], hv.at[pl.ds(0, HOT_CAP)], in_sem.at[5]),
        pltpu.make_async_copy(k_hbm.at[pl.ds(0, HOT_CAP)], hk.at[pl.ds(0, HOT_CAP)], in_sem.at[6]),
        pltpu.make_async_copy(k_hbm, kbuf, in_sem.at[7]),
        pltpu.make_async_copy(v_hbm, vbuf, in_sem.at[8]),
    ]
    for copy in local:
        copy.start()

    barrier = pltpu.get_barrier_semaphore()
    peers = [at(1), at(2), at(3), at(0, 1), at(0, 0, 1)]
    for peer in peers:
        pl.semaphore_signal(barrier, inc=1, device_id=peer, device_id_type=MESH)

    local[0].wait()
    r = lax.broadcasted_iota(I32, (rows, rows), 0)
    col = lax.broadcasted_iota(I32, (rows, rows), 1)
    heads = rows // seqs
    perm = jnp.where(col == (r % seqs) * heads + r // seqs, 1.0, 0.0).astype(BF16)
    q_rows = jnp.dot(perm, q_v[...], preferred_element_type=F32)
    qt[A0] = q_rows.T.astype(BF16)

    pl.semaphore_wait(barrier, len(peers))

    kv_copies = [
        remote(k_hbm.at[pl.ds(0, HOT_CAP)], hk.at[pl.ds(HOT_CAP, HOT_CAP)], kv_send.at[0], kv_recv.at[0], at(0, 0, 1)),
        remote(v_hbm.at[pl.ds(0, HOT_CAP)], hv.at[pl.ds(HOT_CAP, HOT_CAP)], kv_send.at[1], kv_recv.at[1], at(0, 0, 1)),
    ]
    plan = [(A0, B0, (0, 1)), (A0, A3, (1, 0)), (A0, A1, (3, 0)), (A3, A2, (1, 0)), (B0, B3, (1, 0)), (B0, B1, (3, 0)), (B1, B2, (3, 0))]
    gathers = {
        dst: remote(qt.at[src], qt.at[dst], ag_send.at[k], ag_recv.at[k], at(*to))
        for k, (src, dst, to) in enumerate(plan)
    }
    returns = {}
    for k, step in enumerate((A3, A1, A2, B3, B1, B2)):
        dy, dx = OWNER[step]
        slots = rb if dx else ra
        returns[step] = remote(res.at[step], slots.at[NY - dy - 1], rs_send.at[k], rs_recv.at[k], at(dy))
    cross = remote(bsum, rx, rs_send.at[6], rs_recv.at[6], at(0, 1))

    gathers[B0].start()
    gathers[A3].start()
    gathers[A1].start()
    for copy in kv_copies:
        copy.start()

    for copy in local[1:5]:
        copy.wait()
    lane = lax.broadcasted_iota(I32, (2 * seqs, rows), 0)
    pick = lax.broadcasted_iota(I32, (2 * seqs, rows), 1) % seqs
    spread = jnp.where(lane == core * seqs + pick, 1.0, 0.0).astype(BF16)
    used = jnp.dot(used_v[...].astype(F32).astype(BF16), spread, preferred_element_type=F32)
    own_t[pl.ds(0, 8), :] = used
    for step, (dy, dx) in OWNER.items():
        chip = ((y + dy) % NY) * 2 + (xh + dx) % 2
        urow[pl.ds(step, 1), :] = own_t[pl.ds(chip, 1), :]
    lane = lax.broadcasted_iota(I32, (seqs, rows), 0)
    pick = lax.broadcasted_iota(I32, (seqs, rows), 1) % seqs
    spread = jnp.where(lane == pick, 1.0, 0.0).astype(BF16)
    lens = jnp.broadcast_to(len_v[...].astype(F32), (8, seqs)).astype(BF16)
    lrow[...] = jnp.dot(lens, spread, preferred_element_type=F32)
    hot_n = hot_v.shape[1]
    cand = lax.broadcasted_iota(I32, (2 * HOT_CAP, hot_n), 0)
    group = jnp.where(cand < HOT_CAP, me, at(0, 0, 1)["pages"])
    match = hot_v[...] == group * k_hbm.shape[0] + cand % HOT_CAP
    order = lax.broadcasted_iota(I32, (2 * HOT_CAP, hot_n), 1).astype(F32)
    pos[...] = jnp.broadcast_to(
        jnp.min(jnp.where(match, order, 1e9), axis=1, keepdims=True), pos.shape
    )

    qbd[...] = jnp.zeros_like(qbd)

    def set_queries(step):
        qbd[0, pl.ds(0, hd), pl.ds(0, half)] = qt[step, :, pl.ds(0, half)]
        qbd[0, pl.ds(hd, hd), pl.ds(half, half)] = qt[step, :, pl.ds(half, half)]

    def transpose_values(first):
        for j in range(first, first + HOT_CAP):
            for h in range(kvh):
                vt[h, :, pl.ds(j * page, page)] = hv[j, h].T

    local[5].wait()
    transpose_values(0)
    local[6].wait()

    def shared_block(step):
        set_queries(step)
        allowed = jnp.where(urow[pl.ds(step, 1), :] > pos[:, pl.ds(0, 1)], 1.0, 0.0)
        total = jnp.zeros((1, rows), F32)
        parts = [jnp.zeros((hd, half), F32) for _ in range(kvh)]
        for c in range(HOT_CAP):
            keys = jnp.concatenate(
                [hk[pl.ds(2 * c, 2), h].reshape(2 * page, hd) for h in range(kvh)], axis=1
            )
            logits = jnp.dot(keys, qbd[0], preferred_element_type=F32)
            weight = weights_of(logits)
            weight = jnp.concatenate(
                [weight[i * page : (i + 1) * page] * allowed[2 * c + i : 2 * c + i + 1] for i in range(2)], axis=0
            )
            total = total + jnp.sum(weight, axis=0, keepdims=True)
            rounded = weight.astype(BF16)
            for h in range(kvh):
                parts[h] = parts[h] + jnp.dot(
                    vt[h, :, pl.ds(2 * c * page, 2 * page)],
                    rounded[:, h * half : (h + 1) * half],
                    preferred_element_type=F32,
                )
        for h in range(kvh):
            res[step, pl.ds(0, hd), pl.ds(h * half, half)] = parts[h].astype(BF16)
        res[step, pl.ds(hd, 16), :] = split_sum(total, rows)

    def own_scores():
        local[7].wait()
        set_queries(A0)

        def four(g, carry):
            seq_of = lax.broadcasted_iota(I32, (page, rows), 1) % seqs
            tile = own_t[...]
            for i in range(0, 4, 2):
                pages = [up_s[0, g * 4 + i + j] for j in range(2)]
                keys = jnp.concatenate(
                    [jnp.concatenate([kbuf[u, h] for h in range(kvh)], axis=1) for u in pages], axis=0
                )
                logits = jnp.dot(keys, qbd[0], preferred_element_type=F32)
                for j in range(2):
                    tile = jnp.where(seq_of == g * 4 + i + j, logits[j * page : (j + 1) * page], tile)
            own_t[...] = tile
            return carry

        own_t[...] = jnp.zeros_like(own_t)
        lax.fori_loop(0, seqs // 4, four, 0)
        token = lax.broadcasted_iota(I32, (page, rows), 0).astype(F32)
        weight = jnp.where(token < lrow[pl.ds(0, 1), :], weights_of(own_t[...]), 0.0)
        own_t[pl.ds(0, 8), :] = jnp.broadcast_to(jnp.sum(weight, axis=0, keepdims=True), (8, rows))
        own_w[...] = weight.T

    def own_values():
        local[8].wait()
        own_o[...] = jnp.zeros_like(own_o)

        def eight(g, carry):
            seq_of = lax.broadcasted_iota(I32, (rows, page), 0) % seqs
            left, right = [], []
            for i in range(8):
                u = up_s[0, g * 8 + i]
                left.append(jnp.where(seq_of == g * 8 + i, own_w[...], 0.0).astype(BF16))
                right.append(jnp.concatenate([vbuf[u, h] for h in range(kvh)], axis=1))
            own_o[...] += jnp.dot(
                jnp.concatenate(left, axis=1), jnp.concatenate(right, axis=0), preferred_element_type=F32
            )
            return carry

        lax.fori_loop(0, seqs // 8, eight, 0)

    own_scores()
    kv_copies[0].wait()
    kv_copies[1].wait()
    transpose_values(HOT_CAP)

    def one_step(step, carry):
        for k in (A3, A1, A2, B3, B1, B2):
            @pl.when(step == k)
            def _():
                gathers[k].wait_recv()

        @pl.when(step == A3)
        def _():
            gathers[A2].start()

        @pl.when(step == A1)
        def _():
            gathers[B0].wait_recv()
            gathers[B3].start()
            gathers[B1].start()

        @pl.when(step == B1)
        def _():
            gathers[B2].start()

        shared_block(step)
        for k in (A3, A1, A2, B3, B1, B2):
            @pl.when(step == k)
            def _():
                returns[k].start()
        return carry

    lax.fori_loop(0, 8, one_step, 0)
    own_values()

    def summed(pieces):
        return sum(piece[...].astype(F32) for piece in pieces)

    for step in (B3, B1, B2):
        returns[step].wait_recv()
    whole = summed([res.at[B0], rb.at[0], rb.at[1], rb.at[2]])
    bsum[pl.ds(0, hd), :] = whole[:hd].astype(BF16)
    bsum[pl.ds(hd, 16), :] = split_sum(jnp.sum(whole[hd:], axis=0, keepdims=True), rows)
    cross.start()
    own_num = [own_o[pl.ds(h * half, half), pl.ds(h * hd, hd)].T for h in range(kvh)]
    for step in (A3, A1, A2):
        returns[step].wait_recv()
    near = summed([res.at[A0], ra.at[0], ra.at[1], ra.at[2]])
    cross.wait_recv()
    whole = near + rx[...].astype(F32)
    total = jnp.sum(whole[hd:], axis=0, keepdims=True) + own_t[pl.ds(0, 1), :]
    for h in range(kvh):
        lanes = slice(h * half, (h + 1) * half)
        attended = ((whole[:hd, lanes] + own_num[h]) / total[:, lanes]).T.astype(BF16)
        for g in range(half // seqs):
            head = h * (half // seqs) + g
            out_ref[:, pl.ds(head * hd, hd)] = attended[g * seqs : (g + 1) * seqs]

    for copy in gathers.values():
        copy.wait_send()
    for copy in returns.values():
        copy.wait_send()
    cross.wait_send()


def attention(queries, keys, values, hot_pages, hot_used, user_pages, lengths):
    seqs, heads, hd = queries.shape
    pages, kvh, page, _ = keys.shape
    rows = seqs * heads
    half = rows // kvh
    vmem = pltpu.VMEM
    return pl.pallas_call(
        attention_kernel,
        out_shape=jax.ShapeDtypeStruct((seqs, heads * hd), BF16),
        in_specs=[pl.BlockSpec(memory_space=pl.ANY)] * 7,
        out_specs=pl.BlockSpec(memory_space=pltpu.VMEM),
        scratch_shapes=[
            vmem((rows, hd), BF16),
            vmem((1, hot_pages.shape[0]), I32),
            vmem((hot_used.shape[0] // 128, 128), I32),
            vmem((1, seqs), I32),
            pltpu.SMEM((1, seqs), I32),
            vmem((pages, kvh, page, hd), BF16),
            vmem((pages, kvh, page, hd), BF16),
            vmem((2 * HOT_CAP, kvh, page, hd), BF16),
            vmem((2 * HOT_CAP, kvh, page, hd), BF16),
            vmem((kvh, hd, 2 * HOT_CAP * page), BF16),
            vmem((8, hd, rows), BF16),
            vmem((1, kvh * hd, rows), BF16),
            vmem((8, 128), BF16),
            vmem((8, rows), F32),
            vmem((8, rows), F32),
            vmem((2 * HOT_CAP, 128), F32),
            vmem((8, hd + 16, rows), BF16),
            vmem((3, hd + 16, rows), BF16),
            vmem((3, hd + 16, rows), BF16),
            vmem((hd + 16, rows), BF16),
            vmem((hd + 16, rows), BF16),
            vmem((page, rows), F32),
            vmem((rows, page), F32),
            vmem((rows, kvh * hd), F32),
            pltpu.SemaphoreType.DMA((9,)),
            pltpu.SemaphoreType.DMA((2,)),
            pltpu.SemaphoreType.DMA((2,)),
            pltpu.SemaphoreType.DMA((7,)),
            pltpu.SemaphoreType.DMA((7,)),
            pltpu.SemaphoreType.DMA((7,)),
            pltpu.SemaphoreType.DMA((7,)),
        ],
        compiler_params=pltpu.CompilerParams(
            collective_id=0, has_side_effects=True, vmem_limit_bytes=40 * 1024 * 1024
        ),
        name="attention",
    )(
        queries.reshape(rows, hd),
        keys,
        values,
        hot_pages.reshape(1, -1),
        hot_used.reshape(-1, 128),
        user_pages.reshape(1, -1),
        lengths.reshape(1, -1),
    )


def split_up(shard, dim, count):
    shape = shard.shape
    parts = shard.reshape(*shape[:dim], count, shape[dim] // count, *shape[dim + 1 :])
    return jnp.moveaxis(parts, dim, 0)


def sent_and_summed(shard, axis, dim):
    count = lax.axis_size(axis)
    parts = lax.all_to_all(split_up(shard, dim, count), axis, 0, 0, tiled=True)
    return jnp.sum(parts.astype(jnp.float32), axis=0)


def per_device(
    queries, keys, values, hot_pages, hot_used, user_pages, lengths, o_weight, residual, norm_gain
):
    attended = attention(queries, keys, values, hot_pages, hot_used, user_pages, lengths)
    projected = sent_and_summed(
        jnp.dot(attended, o_weight, preferred_element_type=jnp.float32).astype(jnp.bfloat16),
        "heads",
        0,
    )
    mean_sq = jnp.mean(projected * projected, axis=1, keepdims=True)
    normed = projected / jnp.sqrt(mean_sq + epsilon) * norm_gain[None, :]
    return (residual.astype(jnp.float32) + normed).astype(jnp.bfloat16)


def solution(mesh):
    in_specs = (
        P("pages", "heads", None),
        P("pages", "heads", None, None),
        P("pages", "heads", None, None),
        P(),
        P(),
        P("pages", None),
        P("pages"),
        P("heads", None),
        P(("pages", "heads"), None),
        P(),
    )
    out_specs = P(("pages", "heads"), None)
    return jax.shard_map(
        per_device, mesh=mesh, in_specs=in_specs, out_specs=out_specs, check_vma=False
    )
```

time: 107 us -> 56.5 us (0.53)
  Pallas kernels: 0 us -> 31.6 us
  matrix products: 29.6 us -> 0.93 us
  waiting for transfers between devices: 28.2 us -> 0 us
  starting transfers between devices: 11 us -> 0 us
  local copies, waits for them, and re-layouts: 15.5 us -> 8.18 us
  other arithmetic: 5.97 us -> 0.97 us
  blocking collectives: 15.9 us -> 14.2 us
    pallas_call x0 -> x1, Pallas kernels: none -> 31.6 us  [attention(): pl.pallas_call(attention_kernel, out_shape=jax.ShapeDtypeStruct((seqs, he...]
    all_to_all x2 -> x0, waiting for transfers between devices: 28.2 us -> none  [the longest x1 15.5 us: from_everyone(): return lax.all_to_all(copies, axis, split_axis=0, concat_axis=0, tiled=True)]
    dot_general x4 -> x0, matrix products: 26.4 us -> none  [the longest x1 9.23 us: shared_terms(): jnp.einsum('skgd,pktd->skgpt', grouped, page_keys, preferred_element_type...]
    all_to_all x2 -> x0, starting transfers between devices: 11 us -> none  [the longest x1 7.15 us: from_everyone(): return lax.all_to_all(copies, axis, split_axis=0, concat_axis=0, tiled=True)]
    gather x2 -> x0, local copies, waits for them, and re-layouts: 10.8 us -> none  [the longest x1 5.39 us: per_device(): owned_keys = keys[user_pages]]
    unnamed x11 -> x20, local copies, waits for them, and re-layouts: 0.87 us -> 8.18 us
    dot_general x1, matrix products: 3.27 us -> 0.93 us  [per_device(): jnp.dot(attended, o_weight, preferred_element_type=jnp.float32)]
    concatenate x1 -> x0, other arithmetic: 2.05 us -> none  [sent_together(): jnp.concatenate([a.reshape(*a.shape[:along], w) for a, w in zip(arrays, w...]
  transfers between devices with their start and end apart: 2 -> 0, of which waited for: 2 -> 0; matrix products, arithmetic and copies ran while one was open for 18% -> 0% of each run, Pallas kernels for 0% -> 0%
where the time goes in v1:
time: 56.5 us; the launch traced here: 56 us
  Pallas kernels  31.6 us (56%)
  blocking collectives  14.2 us (25%)
  local copies, waits for them, and re-layouts  8.18 us (14%)
  other arithmetic  0.97 us (2%)
  matrix products  0.93 us (2%)
    pallas_call x1, Pallas kernels, attention(): pl.pallas_call(attention_kernel, out_shape=jax.ShapeDtypeStruct((seqs, he...  31.6 us
    all_to_all x1, blocking collectives, sent_and_summed(): parts = lax.all_to_all(split_up(shard, dim, count), axis, 0, 0, tiled=True)  14.2 us
    unnamed x20, local copies, waits for them, and re-layouts  8.18 us

profile of v1, /device:TPU:0, one launch (start us, length us, event | category | flops | bytes accessed | tf_op | source)
XLA Modules:
  0.0 56.0 jit_solution(14521702147083545814)
XLA Ops:
  0.0 0.0 copy-start
  0.0 2.3 %copy-done = bf16[72,2,128,128]{3,2,1,0:T(8,128)(2,1)S(1)} copy-done((bf16[72,2,128,128]{3,2,1,0:T(8,128)(2,1)S(1)}, bf16[72,2,128,128]{3,2,1,0:T(8,128)(2,1)}, u32[]{:S(2)}) %copy-start) | copy-done | bytes 4718616
  2.3 0.0 copy-start.1
  2.3 2.3 %copy-done.1 = bf16[72,2,128,128]{3,2,1,0:T(8,128)(2,1)S(1)} copy-done((bf16[72,2,128,128]{3,2,1,0:T(8,128)(2,1)S(1)}, bf16[72,2,128,128]{3,2,1,0:T(8,128)(2,1)}, u32[]{:S(2)}) %copy-start.1) | copy-done | bytes 4718616
  4.7 0.0 copy-start.2
  4.7 0.8 %copy-done.2 = bf16[64,4,128]{2,1,0:T(4,128)(2,1)S(1)} copy-done((bf16[64,4,128]{2,1,0:T(4,128)(2,1)S(1)}, bf16[64,4,128]{2,1,0:T(4,128)(2,1)}, u32[]{:S(2)}) %copy-start.2) | copy-done | bytes 65560
  5.5 0.0 copy-start.3
  5.5 0.7 %copy-done.3 = s32[1024]{0:T(1024)S(1)} copy-done((s32[1024]{0:T(1024)S(1)}, s32[1024]{0:T(1024)}, u32[]{:S(2)}) %copy-start.3) | copy-done | bytes 4120
  6.2 0.0 copy-start.4
  6.2 0.7 %copy-done.4 = s32[64]{0:T(128)S(1)} copy-done((s32[64]{0:T(128)S(1)}, s32[64]{0:T(128)}, u32[]{:S(2)}) %copy-start.4) | copy-done | bytes 280
  6.9 0.0 copy-start.5
  6.9 0.7 %copy-done.5 = s32[64,1]{0,1:T(1,128)S(1)} copy-done((s32[64,1]{0,1:T(1,128)S(1)}, s32[64,1]{0,1:T(1,128)}, u32[]{:S(2)}) %copy-start.5) | copy-done | bytes 280
  7.5 0.0 copy-start.6
  7.5 0.7 %copy-done.6 = s32[64]{0:T(128)S(1)} copy-done((s32[64]{0:T(128)S(1)}, s32[64]{0:T(128)}, u32[]{:S(2)}) %copy-start.6) | copy-done | bytes 280
  8.2 0.0 copy-start.7
  8.2 31.6 %attention.1 = bf16[64,512]{1,0:T(8,128)(2,1)S(1)} custom-call(bf16[256,128]{1,0:T(8,128)(2,1)S(1)} %bitcast.9, bf16[72,2,128,128]{3,2,1,0:T(8,128)(2,1)S(1)} %copy-done, bf16[72,2,128,128]{3,2,1,0:T(8,128)(2,1)S(1)} %copy-done.1, s32[1,64]{1,0:T(1,128)S(1)} %bitcast.11, s32[8,128]{1,0:T(8,128)S(1)} %bitcast.10, s32[1,64]{1,0:T(1,128)S(1)} %bitcast.12, ...), custom_call_target="tpu_custom_call" | custom-call | tf_op jit(solution)/shard_map/attention/pallas_call | solution.py:284
  39.8 0.0 copy-done.7
  39.8 0.0 copy-start.8
  39.8 0.0 copy-start.9
  39.8 0.9 %fusion = bf16[8,8,4608]{2,1,0:T(8,128)(2,1)S(1)} fusion(bf16[64,512]{1,0:T(8,128)(2,1)S(1)} %attention.1, bf16[512,4608]{1,0:T(8,128)(2,1)S(1)} %copy-done.7), kind=kOutput, calls=%fused_computation.1 | convolution fusion | flops 302284800 | bytes 5373952 | tf_op jit(solution)/shard_map/dot_general | solution.py:354
  40.7 14.2 %all_to_all.5 = bf16[8,8,4608]{2,1,0:T(8,128)(2,1)S(1)} all-to-all(bf16[8,8,4608]{2,1,0:T(8,128)(2,1)S(1)} %fusion), channel_id=1, replica_groups=mesh['pages'=16,'heads'=8] {'heads'}, dimensions={0} | all-to-all | bytes 1179648 | tf_op jit(solution)/shard_map/all_to_all | solution.py:345
  55.0 0.1 convert_reduce_fusion
  55.1 0.2 multiply_reduce_fusion
  55.2 0.0 copy-done.8
  55.2 0.0 copy-done.9
  55.2 0.7 %add_convert_fusion = bf16[8,4608]{1,0:T(8,128)(2,1)} fusion(f32[8,4608]{1,0:T(8,128)S(1)} %convert_reduce_fusion, bf16[8,4608]{1,0:T(8,128)(2,1)S(1)} %copy-done.8, f32[4608]{0:T(1024)S(1)} %copy-done.9, f32[8]{0:T(128)S(1)} %add_sqrt_fusion), kind=kLoop, calls=%fused_computation.3 | loop fusion | flops 184320 | bytes 313376 | tf_op jit(solution)/shard_map/convert_element_type | solution.py:360
  (1 shorter events, 0.0 us)
Async XLA Ops:
  0.0 2.3 %copy-start = (bf16[72,2,128,128]{3,2,1,0:T(8,128)(2,1)S(1)}, bf16[72,2,128,128]{3,2,1,0:T(8,128)(2,1)}, u32[]{:S(2)}) copy-start(bf16[72,2,128,128]{3,2,1,0:T(8,128)(2,1)} %k_hbm.1) | copy-start | bytes 14155780
  2.3 2.3 %copy-start.1 = (bf16[72,2,128,128]{3,2,1,0:T(8,128)(2,1)S(1)}, bf16[72,2,128,128]{3,2,1,0:T(8,128)(2,1)}, u32[]{:S(2)}) copy-start(bf16[72,2,128,128]{3,2,1,0:T(8,128)(2,1)} %v_hbm.1) | copy-start | bytes 14155780
  4.7 0.8 %copy-start.2 = (bf16[64,4,128]{2,1,0:T(4,128)(2,1)S(1)}, bf16[64,4,128]{2,1,0:T(4,128)(2,1)}, u32[]{:S(2)}) copy-start(bf16[64,4,128]{2,1,0:T(4,128)(2,1)} %param.10) | copy-start | bytes 196612
  5.5 0.7 %copy-start.3 = (s32[1024]{0:T(1024)S(1)}, s32[1024]{0:T(1024)}, u32[]{:S(2)}) copy-start(s32[1024]{0:T(1024)} %param.14) | copy-start | bytes 12292
  6.2 0.7 %copy-start.4 = (s32[64]{0:T(128)S(1)}, s32[64]{0:T(128)}, u32[]{:S(2)}) copy-start(s32[64]{0:T(128)} %param.13) | copy-start | bytes 772
  6.9 0.7 %copy-start.5 = (s32[64,1]{0,1:T(1,128)S(1)}, s32[64,1]{0,1:T(1,128)}, u32[]{:S(2)}) copy-start(s32[64,1]{0,1:T(1,128)} %param.15) | copy-start | bytes 772
  7.5 0.7 %copy-start.6 = (s32[64]{0:T(128)S(1)}, s32[64]{0:T(128)}, u32[]{:S(2)}) copy-start(s32[64]{0:T(128)} %param.16) | copy-start | bytes 772
  8.2 31.6 %copy-start.7 = (bf16[512,4608]{1,0:T(8,128)(2,1)S(1)}, bf16[512,4608]{1,0:T(8,128)(2,1)}, u32[]{:S(2)}) copy-start(bf16[512,4608]{1,0:T(8,128)(2,1)} %param.17) | copy-start | bytes 14155780
  39.8 15.5 %copy-start.8 = (bf16[8,4608]{1,0:T(8,128)(2,1)S(1)}, bf16[8,4608]{1,0:T(8,128)(2,1)}, u32[]{:S(2)}) copy-start(bf16[8,4608]{1,0:T(8,128)(2,1)} %param.18) | copy-start | bytes 221188
  39.8 15.4 %copy-start.9 = (f32[4608]{0:T(1024)S(1)}, f32[4608]{0:T(1024)}, u32[]{:S(2)}) copy-start(f32[4608]{0:T(1024)} %param.19) | copy-start | bytes 55300

commit v2 on v1

--- a/solution.py
+++ b/solution.py
@@ -13,6 +13,8 @@
 score_scale = 1.0 / 12.0
 epsilon = 1e-06
 NY = 4
+NZ = 4
+CHUNKS = 3
 F32, BF16, I32 = jnp.float32, jnp.bfloat16, jnp.int32
 MESH = pl.DeviceIdType.MESH
 
@@ -30,11 +32,12 @@
     return jnp.where(row == 0, high, jnp.where(row == 1, totals - high, 0.0)).astype(BF16)
 
 
-def attention_kernel(
-    q_hbm, k_hbm, v_hbm, hot_hbm, used_hbm, up_hbm, len_hbm, out_ref,
-    q_v, hot_v, used_v, len_v, up_s, kbuf, vbuf, hk, hv, vt, qt, qbd, wt, urow, lrow, pos,
+def layer_kernel(
+    q_hbm, k_hbm, v_hbm, hot_hbm, used_hbm, up_hbm, len_hbm, w_hbm, out_ref,
+    q_v, hot_v, used_v, len_v, up_s, kbuf, vbuf, hk, hv, vt, qt, qbd, urow, lrow, pos,
     res, ra, rb, rx, bsum, own_t, own_w, own_o,
-    in_sem, kv_send, kv_recv, ag_send, ag_recv, rs_send, rs_recv,
+    w_v, att, pz, zr, px, xr, near_sum,
+    in_sem, z_send, z_recv, x_send, x_recv, kv_send, kv_recv, ag_send, ag_recv, rs_send, rs_recv,
 ):
     seqs = len_v.shape[1]
     kvh, page, hd = hk.shape[1:]
@@ -42,6 +45,15 @@
     half = rows // kvh
     me = lax.axis_index("pages")
     y, xh, core = me // 4, (me // 2) % 2, me % 2
+
+    member = lax.axis_index("heads")
+    xl, z = member // NZ, member % NZ
+
+    def head_at(dx, dz):
+        return {"heads": ((xl + dx) % 2) * NZ + (z + dz) % NZ}
+
+    def seq_at(place):
+        return ((place // 8) % 2) * (seqs // 2) + (place // 16) * 8 + place % 8
 
     def at(dy, dx=0, dc=0):
         return {"pages": ((y + dy) % NY) * 4 + ((xh + dx) % 2) * 2 + (core + dc) % 2}
@@ -61,12 +73,14 @@
         pltpu.make_async_copy(k_hbm.at[pl.ds(0, HOT_CAP)], hk.at[pl.ds(0, HOT_CAP)], in_sem.at[6]),
         pltpu.make_async_copy(k_hbm, kbuf, in_sem.at[7]),
         pltpu.make_async_copy(v_hbm, vbuf, in_sem.at[8]),
+        pltpu.make_async_copy(w_hbm, w_v, in_sem.at[9]),
     ]
     for copy in local:
         copy.start()
 
     barrier = pltpu.get_barrier_semaphore()
     peers = [at(1), at(2), at(3), at(0, 1), at(0, 0, 1)]
+    peers += [head_at(0, 1), head_at(0, 2), head_at(0, 3), head_at(1, 0)]
     for peer in peers:
         pl.semaphore_signal(barrier, inc=1, device_id=peer, device_id_type=MESH)
 
@@ -74,7 +88,7 @@
     r = lax.broadcasted_iota(I32, (rows, rows), 0)
     col = lax.broadcasted_iota(I32, (rows, rows), 1)
     heads = rows // seqs
-    perm = jnp.where(col == (r % seqs) * heads + r // seqs, 1.0, 0.0).astype(BF16)
+    perm = jnp.where(col == seq_at(r % seqs) * heads + r // seqs, 1.0, 0.0).astype(BF16)
     q_rows = jnp.dot(perm, q_v[...], preferred_element_type=F32)
     qt[A0] = q_rows.T.astype(BF16)
 
@@ -105,7 +119,7 @@
     for copy in local[1:5]:
         copy.wait()
     lane = lax.broadcasted_iota(I32, (2 * seqs, rows), 0)
-    pick = lax.broadcasted_iota(I32, (2 * seqs, rows), 1) % seqs
+    pick = seq_at(lax.broadcasted_iota(I32, (2 * seqs, rows), 1) % seqs)
     spread = jnp.where(lane == core * seqs + pick, 1.0, 0.0).astype(BF16)
     used = jnp.dot(used_v[...].astype(F32).astype(BF16), spread, preferred_element_type=F32)
     own_t[pl.ds(0, 8), :] = used
@@ -113,7 +127,7 @@
         chip = ((y + dy) % NY) * 2 + (xh + dx) % 2
         urow[pl.ds(step, 1), :] = own_t[pl.ds(chip, 1), :]
     lane = lax.broadcasted_iota(I32, (seqs, rows), 0)
-    pick = lax.broadcasted_iota(I32, (seqs, rows), 1) % seqs
+    pick = seq_at(lax.broadcasted_iota(I32, (seqs, rows), 1) % seqs)
     spread = jnp.where(lane == pick, 1.0, 0.0).astype(BF16)
     lens = jnp.broadcast_to(len_v[...].astype(F32), (8, seqs)).astype(BF16)
     lrow[...] = jnp.dot(lens, spread, preferred_element_type=F32)
@@ -175,7 +189,7 @@
             seq_of = lax.broadcasted_iota(I32, (page, rows), 1) % seqs
             tile = own_t[...]
             for i in range(0, 4, 2):
-                pages = [up_s[0, g * 4 + i + j] for j in range(2)]
+                pages = [up_s[0, seq_at(g * 4 + i + j)] for j in range(2)]
                 keys = jnp.concatenate(
                     [jnp.concatenate([kbuf[u, h] for h in range(kvh)], axis=1) for u in pages], axis=0
                 )
@@ -200,7 +214,7 @@
             seq_of = lax.broadcasted_iota(I32, (rows, page), 0) % seqs
             left, right = [], []
             for i in range(8):
-                u = up_s[0, g * 8 + i]
+                u = up_s[0, seq_at(g * 8 + i)]
                 left.append(jnp.where(seq_of == g * 8 + i, own_w[...], 0.0).astype(BF16))
                 right.append(jnp.concatenate([vbuf[u, h] for h in range(kvh)], axis=1))
             own_o[...] += jnp.dot(
@@ -266,25 +280,61 @@
         attended = ((whole[:hd, lanes] + own_num[h]) / total[:, lanes]).T.astype(BF16)
         for g in range(half // seqs):
             head = h * (half // seqs) + g
-            out_ref[:, pl.ds(head * hd, hd)] = attended[g * seqs : (g + 1) * seqs]
-
-    for copy in gathers.values():
+            att[:, pl.ds(head * hd, hd)] = attended[g * seqs : (g + 1) * seqs]
+
+    local[9].wait()
+    block = seqs // NZ
+    width = w_v.shape[1] // CHUNKS
+    to_z, to_x = [], []
+    for k in range(CHUNKS):
+        cols = pl.ds(k * width, width)
+        piece = jnp.dot(att[...], w_v[:, cols], preferred_element_type=F32).astype(BF16)
+        for i in range(NZ):
+            pz[i, :, cols] = piece[i * block : (i + 1) * block]
+        copies = []
+        for d in (1, 3, 2):
+            n = k * 3 + d - 1
+            copies.append(
+                remote(pz.at[(z + d) % NZ, :, cols], zr.at[NZ - d - 1, :, cols], z_send.at[n], z_recv.at[n], head_at(0, d))
+            )
+            copies[-1].start()
+        to_z.append(copies)
+    for k in range(CHUNKS):
+        cols = pl.ds(k * width, width)
+        for copy in to_z[k]:
+            copy.wait_recv()
+        both = pz[z, :, cols].astype(F32)
+        for i in range(NZ - 1):
+            both = both + zr[i, :, cols].astype(F32)
+        first, second = both[: block // 2], both[block // 2 :]
+        near_sum[:, cols] = jnp.where(xl == 0, first, second)
+        px[:, cols] = jnp.where(xl == 0, second, first).astype(BF16)
+        copy = remote(px.at[:, cols], xr.at[:, cols], x_send.at[k], x_recv.at[k], head_at(1, 0))
+        copy.start()
+        to_x.append(copy)
+    square = jnp.zeros((block // 2, 1), F32)
+    for k in range(CHUNKS):
+        cols = pl.ds(k * width, width)
+        to_x[k].wait_recv()
+        projected = near_sum[:, cols] + xr[:, cols].astype(F32)
+        near_sum[:, cols] = projected
+        square = square + jnp.sum(projected * projected, axis=1, keepdims=True)
+    out_ref[...] = near_sum[...] / jnp.sqrt(square / w_v.shape[1] + epsilon)
+
+    for copy in (*gathers.values(), *returns.values(), cross, *sum(to_z, []), *to_x):
         copy.wait_send()
-    for copy in returns.values():
-        copy.wait_send()
-    cross.wait_send()
-
-
-def attention(queries, keys, values, hot_pages, hot_used, user_pages, lengths):
+
+
+def layer(queries, keys, values, hot_pages, hot_used, user_pages, lengths, o_weight):
     seqs, heads, hd = queries.shape
     pages, kvh, page, _ = keys.shape
     rows = seqs * heads
-    half = rows // kvh
+    width = o_weight.shape[1]
     vmem = pltpu.VMEM
     return pl.pallas_call(
-        attention_kernel,
-        out_shape=jax.ShapeDtypeStruct((seqs, heads * hd), BF16),
-        in_specs=[pl.BlockSpec(memory_space=pl.ANY)] * 7,
+        layer_kernel,
+        out_shape=jax.ShapeDtypeStruct((seqs // 8, width), F32),
+        in_specs=[pl.BlockSpec(memory_space=pl.ANY)] * 8,
         out_specs=pl.BlockSpec(memory_space=pltpu.VMEM),
         scratch_shapes=[
             vmem((rows, hd), BF16),
@@ -299,7 +349,6 @@
             vmem((kvh, hd, 2 * HOT_CAP * page), BF16),
             vmem((8, hd, rows), BF16),
             vmem((1, kvh * hd, rows), BF16),
-            vmem((8, 128), BF16),
             vmem((8, rows), F32),
             vmem((8, rows), F32),
             vmem((2 * HOT_CAP, 128), F32),
@@ -311,7 +360,18 @@
             vmem((page, rows), F32),
             vmem((rows, page), F32),
             vmem((rows, kvh * hd), F32),
-            pltpu.SemaphoreType.DMA((9,)),
+            vmem(o_weight.shape, BF16),
+            vmem((seqs, heads * hd), BF16),
+            vmem((NZ, seqs // NZ, width), BF16),
+            vmem((NZ - 1, seqs // NZ, width), BF16),
+            vmem((seqs // 8, width), BF16),
+            vmem((seqs // 8, width), BF16),
+            vmem((seqs // 8, width), F32),
+            pltpu.SemaphoreType.DMA((10,)),
+            pltpu.SemaphoreType.DMA((3 * CHUNKS,)),
+            pltpu.SemaphoreType.DMA((3 * CHUNKS,)),
+            pltpu.SemaphoreType.DMA((CHUNKS,)),
+            pltpu.SemaphoreType.DMA((CHUNKS,)),
             pltpu.SemaphoreType.DMA((2,)),
             pltpu.SemaphoreType.DMA((2,)),
             pltpu.SemaphoreType.DMA((7,)),
@@ -320,9 +380,9 @@
             pltpu.SemaphoreType.DMA((7,)),
         ],
         compiler_params=pltpu.CompilerParams(
-            collective_id=0, has_side_effects=True, vmem_limit_bytes=40 * 1024 * 1024
+            collective_id=0, has_side_effects=True, vmem_limit_bytes=66_000_000
         ),
-        name="attention",
+        name="layer",
     )(
         queries.reshape(rows, hd),
         keys,
@@ -331,33 +391,15 @@
         hot_used.reshape(-1, 128),
         user_pages.reshape(1, -1),
         lengths.reshape(1, -1),
+        o_weight,
     )
-
-
-def split_up(shard, dim, count):
-    shape = shard.shape
-    parts = shard.reshape(*shape[:dim], count, shape[dim] // count, *shape[dim + 1 :])
-    return jnp.moveaxis(parts, dim, 0)
-
-
-def sent_and_summed(shard, axis, dim):
-    count = lax.axis_size(axis)
-    parts = lax.all_to_all(split_up(shard, dim, count), axis, 0, 0, tiled=True)
-    return jnp.sum(parts.astype(jnp.float32), axis=0)
 
 
 def per_device(
     queries, keys, values, hot_pages, hot_used, user_pages, lengths, o_weight, residual, norm_gain
 ):
-    attended = attention(queries, keys, values, hot_pages, hot_used, user_pages, lengths)
-    projected = sent_and_summed(
-        jnp.dot(attended, o_weight, preferred_element_type=jnp.float32).astype(jnp.bfloat16),
-        "heads",
-        0,
-    )
-    mean_sq = jnp.mean(projected * projected, axis=1, keepdims=True)
-    normed = projected / jnp.sqrt(mean_sq + epsilon) * norm_gain[None, :]
-    return (residual.astype(jnp.float32) + normed).astype(jnp.bfloat16)
+    normed = layer(queries, keys, values, hot_pages, hot_used, user_pages, lengths, o_weight)
+    return (residual.astype(F32) + normed * norm_gain[None, :]).astype(BF16)
 
 
 def solution(mesh):

time: 56.5 us -> 47.4 us (0.84)
  blocking collectives: 14.2 us -> 0 us
  Pallas kernels: 31.6 us -> 45.6 us
  local copies, waits for them, and re-layouts: 8.18 us -> 0.01 us
  matrix products: 0.93 us -> 0 us
  other arithmetic: 0.97 us -> 1.57 us
    all_to_all x1 -> x0, blocking collectives: 14.2 us -> none  [sent_and_summed(): parts = lax.all_to_all(split_up(shard, dim, count), axis, 0, 0, tiled=True)]
    pallas_call x1, Pallas kernels: 31.6 us -> 45.6 us  [layer(): pl.pallas_call(layer_kernel, out_shape=jax.ShapeDtypeStruct((seqs // 8, w...]
    unnamed x20 -> x4, local copies, waits for them, and re-layouts: 8.18 us -> 0.01 us
    dot_general x1 -> x0, matrix products: 0.93 us -> none  [per_device(): jnp.dot(attended, o_weight, preferred_element_type=jnp.float32)]
    convert_element_type x1, other arithmetic: 0.73 us -> 1.57 us  [per_device(): return (residual.astype(F32) + normed * norm_gain[None, :]).astype(BF16)]
where the time goes in v2:
time: 47.4 us; the launch traced here: 47.2 us
  Pallas kernels  45.6 us (96%)
  other arithmetic  1.57 us (3%)
    pallas_call x1, Pallas kernels, layer(): pl.pallas_call(layer_kernel, out_shape=jax.ShapeDtypeStruct((seqs // 8, w...  45.6 us
    convert_element_type x1, other arithmetic, per_device(): return (residual.astype(F32) + normed * norm_gain[None, :]).astype(BF16)  1.57 us

profile of v2, /device:TPU:0, one launch (start us, length us, event | category | flops | bytes accessed | tf_op | source)
XLA Modules:
  0.0 47.2 jit_solution(13336753120527264622)
XLA Ops:
  0.0 0.0 copy-start
  0.0 0.0 copy-start.1
  0.0 45.6 %layer.1 = f32[8,4608]{1,0:T(8,128)} custom-call(bf16[256,128]{1,0:T(8,128)(2,1)} %bitcast.5, bf16[72,2,128,128]{3,2,1,0:T(8,128)(2,1)} %k_hbm.1, bf16[72,2,128,128]{3,2,1,0:T(8,128)(2,1)} %v_hbm.1, s32[1,64]{1,0:T(1,128)} %bitcast.7, s32[8,128]{1,0:T(8,128)} %bitcast.6, s32[1,64]{1,0:T(1,128)} %bitcast.8, s32[1,64]{1,0:T(1,128)} %bitcast.9, ...), custom_call_target="tpu_custom_call" | custom-call | tf_op jit(solution)/shard_map/layer/pallas_call | solution.py:334
  45.7 0.0 copy-done
  45.7 0.0 copy-done.1
  45.7 1.6 %add_convert_fusion = bf16[8,4608]{1,0:T(8,128)(2,1)} fusion(f32[8,4608]{1,0:T(8,128)} %layer.1, bf16[8,4608]{1,0:T(8,128)(2,1)S(1)} %copy-done, f32[4608]{0:T(1024)S(1)} %copy-done.1), kind=kLoop, calls=%fused_computation | loop fusion | flops 147456 | bytes 313344 | tf_op jit(solution)/shard_map/convert_element_type | solution.py:402
Async XLA Ops:
  0.0 45.7 %copy-start = (bf16[8,4608]{1,0:T(8,128)(2,1)S(1)}, bf16[8,4608]{1,0:T(8,128)(2,1)}, u32[]{:S(2)}) copy-start(bf16[8,4608]{1,0:T(8,128)(2,1)} %param.18) | copy-start | bytes 221188
  0.0 45.7 %copy-start.1 = (f32[4608]{0:T(1024)S(1)}, f32[4608]{0:T(1024)}, u32[]{:S(2)}) copy-start(f32[4608]{0:T(1024)} %param.19) | copy-start | bytes 55300

commit v3 on v2

--- a/solution.py
+++ b/solution.py
@@ -14,12 +14,12 @@
 epsilon = 1e-06
 NY = 4
 NZ = 4
-CHUNKS = 3
+CHUNKS = 4
 F32, BF16, I32 = jnp.float32, jnp.bfloat16, jnp.int32
 MESH = pl.DeviceIdType.MESH
 
-A0, A3, A1, A2, B3, B1, B2, B0 = range(8)
-OWNER = {A0: (0, 0), A3: (3, 0), A1: (1, 0), A2: (2, 0), B3: (3, 1), B1: (1, 1), B2: (2, 1), B0: (0, 1)}
+A3, A1, A2, B0, B3, B1, B2, A0 = range(8)
+OWNER = {A3: (3, 0), A1: (1, 0), A2: (2, 0), B0: (0, 1), B3: (3, 1), B1: (1, 1), B2: (2, 1), A0: (0, 0)}
 
 
 def weights_of(logits):
@@ -35,9 +35,9 @@
 def layer_kernel(
     q_hbm, k_hbm, v_hbm, hot_hbm, used_hbm, up_hbm, len_hbm, w_hbm, out_ref,
     q_v, hot_v, used_v, len_v, up_s, kbuf, vbuf, hk, hv, vt, qt, qbd, urow, lrow, pos,
-    res, ra, rb, rx, bsum, own_t, own_w, own_o,
-    w_v, att, pz, zr, px, xr, near_sum,
-    in_sem, z_send, z_recv, x_send, x_recv, kv_send, kv_recv, ag_send, ag_recv, rs_send, rs_recv,
+    res, ra, own_t, own_w, own_o,
+    w_v, att, pz, zt, zj, zr, px, xr, near_sum,
+    in_sem, z_send, z_recv, x_send, x_recv, kv_send, kv_recv, ag_send, ag_recv, rs_send, rs_recv, far_sem,
 ):
     seqs = len_v.shape[1]
     kvh, page, hd = hk.shape[1:]
@@ -63,19 +63,21 @@
             src_ref=src, dst_ref=dst, send_sem=send, recv_sem=recv, device_id=target, device_id_type=MESH
         )
 
+    own = pl.ds(HOT_CAP, k_hbm.shape[0] - HOT_CAP)
+    hot = pl.ds(0, HOT_CAP)
     local = [
         pltpu.make_async_copy(q_hbm, q_v, in_sem.at[0]),
         pltpu.make_async_copy(hot_hbm, hot_v, in_sem.at[1]),
         pltpu.make_async_copy(used_hbm, used_v, in_sem.at[2]),
         pltpu.make_async_copy(len_hbm, len_v, in_sem.at[3]),
         pltpu.make_async_copy(up_hbm, up_s, in_sem.at[4]),
-        pltpu.make_async_copy(v_hbm.at[pl.ds(0, HOT_CAP)], hv.at[pl.ds(0, HOT_CAP)], in_sem.at[5]),
-        pltpu.make_async_copy(k_hbm.at[pl.ds(0, HOT_CAP)], hk.at[pl.ds(0, HOT_CAP)], in_sem.at[6]),
-        pltpu.make_async_copy(k_hbm, kbuf, in_sem.at[7]),
-        pltpu.make_async_copy(v_hbm, vbuf, in_sem.at[8]),
+        pltpu.make_async_copy(k_hbm.at[hot], hk.at[hot], in_sem.at[5]),
+        pltpu.make_async_copy(v_hbm.at[hot], hv.at[hot], in_sem.at[6]),
+        pltpu.make_async_copy(k_hbm.at[own], kbuf, in_sem.at[7]),
+        pltpu.make_async_copy(v_hbm.at[own], vbuf, in_sem.at[8]),
         pltpu.make_async_copy(w_hbm, w_v, in_sem.at[9]),
     ]
-    for copy in local:
+    for copy in local[:8]:
         copy.start()
 
     barrier = pltpu.get_barrier_semaphore()
@@ -94,27 +96,31 @@
 
     pl.semaphore_wait(barrier, len(peers))
 
+    far = pl.ds(HOT_CAP, HOT_CAP)
     kv_copies = [
-        remote(k_hbm.at[pl.ds(0, HOT_CAP)], hk.at[pl.ds(HOT_CAP, HOT_CAP)], kv_send.at[0], kv_recv.at[0], at(0, 0, 1)),
-        remote(v_hbm.at[pl.ds(0, HOT_CAP)], hv.at[pl.ds(HOT_CAP, HOT_CAP)], kv_send.at[1], kv_recv.at[1], at(0, 0, 1)),
+        remote(hk.at[hot], hk.at[far], kv_send.at[0], kv_recv.at[0], at(0, 0, 1)),
+        remote(hv.at[hot], hv.at[far], kv_send.at[1], kv_recv.at[1], at(0, 0, 1)),
     ]
-    plan = [(A0, B0, (0, 1)), (A0, A3, (1, 0)), (A0, A1, (3, 0)), (A3, A2, (1, 0)), (B0, B3, (1, 0)), (B0, B1, (3, 0)), (B1, B2, (3, 0))]
-    gathers = {
-        dst: remote(qt.at[src], qt.at[dst], ag_send.at[k], ag_recv.at[k], at(*to))
-        for k, (src, dst, to) in enumerate(plan)
+    gathers, returns = {}, {}
+    for step, (dy, dx) in OWNER.items():
+        if step == A0:
+            continue
+        back = next(k for k, at_ in OWNER.items() if at_ == ((NY - dy) % NY, dx))
+        gathers[step] = remote(qt.at[A0], qt.at[step], ag_send.at[step], ag_recv.at[step], at((NY - dy) % NY, dx))
+        returns[step] = remote(res.at[step], ra.at[back], rs_send.at[step], rs_recv.at[back], at(dy, dx))
+    arrivals = {
+        step: remote(res.at[step], ra.at[step], rs_send.at[step], rs_recv.at[step], at(0, 1)) for step in returns
     }
-    returns = {}
-    for k, step in enumerate((A3, A1, A2, B3, B1, B2)):
-        dy, dx = OWNER[step]
-        slots = rb if dx else ra
-        returns[step] = remote(res.at[step], slots.at[NY - dy - 1], rs_send.at[k], rs_recv.at[k], at(dy))
-    cross = remote(bsum, rx, rs_send.at[6], rs_recv.at[6], at(0, 1))
-
-    gathers[B0].start()
-    gathers[A3].start()
-    gathers[A1].start()
+
+    pl.semaphore_signal(far_sem, inc=1, device_id=at(0, 1), device_id_type=MESH)
+    for step in (A3, A1, A2, B0):
+        gathers[step].start()
+    local[5].wait()
+    local[6].wait()
     for copy in kv_copies:
         copy.start()
+    local[8].start()
+    local[9].start()
 
     for copy in local[1:5]:
         copy.wait()
@@ -151,9 +157,7 @@
             for h in range(kvh):
                 vt[h, :, pl.ds(j * page, page)] = hv[j, h].T
 
-    local[5].wait()
     transpose_values(0)
-    local[6].wait()
 
     def shared_block(step):
         set_queries(step)
@@ -181,26 +185,31 @@
             res[step, pl.ds(0, hd), pl.ds(h * half, half)] = parts[h].astype(BF16)
         res[step, pl.ds(hd, 16), :] = split_sum(total, rows)
 
+    def page_of(place):
+        return jnp.maximum(up_s[0, seq_at(place)] - HOT_CAP, 0)
+
     def own_scores():
         local[7].wait()
         set_queries(A0)
 
-        def four(g, carry):
+        def some(g, carry):
             seq_of = lax.broadcasted_iota(I32, (page, rows), 1) % seqs
             tile = own_t[...]
-            for i in range(0, 4, 2):
-                pages = [up_s[0, seq_at(g * 4 + i + j)] for j in range(2)]
+            for i in range(0, 16, 2):
+                pages = [page_of(g * 16 + i + j) for j in range(2)]
                 keys = jnp.concatenate(
                     [jnp.concatenate([kbuf[u, h] for h in range(kvh)], axis=1) for u in pages], axis=0
                 )
                 logits = jnp.dot(keys, qbd[0], preferred_element_type=F32)
                 for j in range(2):
-                    tile = jnp.where(seq_of == g * 4 + i + j, logits[j * page : (j + 1) * page], tile)
+                    tile = jnp.where(seq_of == g * 16 + i + j, logits[j * page : (j + 1) * page], tile)
             own_t[...] = tile
             return carry
 
         own_t[...] = jnp.zeros_like(own_t)
-        lax.fori_loop(0, seqs // 4, four, 0)
+        lax.fori_loop(0, seqs // 16, some, 0)
+
+    def own_weights():
         token = lax.broadcasted_iota(I32, (page, rows), 0).astype(F32)
         weight = jnp.where(token < lrow[pl.ds(0, 1), :], weights_of(own_t[...]), 0.0)
         own_t[pl.ds(0, 8), :] = jnp.broadcast_to(jnp.sum(weight, axis=0, keepdims=True), (8, rows))
@@ -208,49 +217,43 @@
 
     def own_values():
         local[8].wait()
-        own_o[...] = jnp.zeros_like(own_o)
-
-        def eight(g, carry):
-            seq_of = lax.broadcasted_iota(I32, (rows, page), 0) % seqs
-            left, right = [], []
-            for i in range(8):
-                u = up_s[0, seq_at(g * 8 + i)]
-                left.append(jnp.where(seq_of == g * 8 + i, own_w[...], 0.0).astype(BF16))
-                right.append(jnp.concatenate([vbuf[u, h] for h in range(kvh)], axis=1))
-            own_o[...] += jnp.dot(
-                jnp.concatenate(left, axis=1), jnp.concatenate(right, axis=0), preferred_element_type=F32
-            )
+
+        def some(n, carry):
+            row = lax.broadcasted_iota(I32, (8 * heads, page), 0) % 8
+            for m in range(4):
+                g = n * 4 + m
+                weight = jnp.concatenate([own_w[pl.ds(h * seqs + g * 8, 8), :] for h in range(heads)], axis=0)
+                left, right = [], []
+                for i in range(8):
+                    u = page_of(g * 8 + i)
+                    left.append(jnp.where(row == i, weight, 0.0).astype(BF16))
+                    right.append(jnp.concatenate([vbuf[u, h] for h in range(kvh)], axis=1))
+                part = jnp.dot(
+                    jnp.concatenate(left, axis=1), jnp.concatenate(right, axis=0), preferred_element_type=F32
+                )
+                for h in range(heads):
+                    own_o[pl.ds(h * seqs + g * 8, 8), :] = part[h * 8 : (h + 1) * 8]
             return carry
 
-        lax.fori_loop(0, seqs // 8, eight, 0)
+        lax.fori_loop(0, seqs // 32, some, 0)
 
     own_scores()
+    pl.semaphore_wait(far_sem, 1)
+    for step in (B3, B1, B2):
+        gathers[step].start()
+    own_weights()
     kv_copies[0].wait()
     kv_copies[1].wait()
     transpose_values(HOT_CAP)
 
     def one_step(step, carry):
-        for k in (A3, A1, A2, B3, B1, B2):
+        for k in gathers:
             @pl.when(step == k)
             def _():
                 gathers[k].wait_recv()
 
-        @pl.when(step == A3)
-        def _():
-            gathers[A2].start()
-
-        @pl.when(step == A1)
-        def _():
-            gathers[B0].wait_recv()
-            gathers[B3].start()
-            gathers[B1].start()
-
-        @pl.when(step == B1)
-        def _():
-            gathers[B2].start()
-
         shared_block(step)
-        for k in (A3, A1, A2, B3, B1, B2):
+        for k in returns:
             @pl.when(step == k)
             def _():
                 returns[k].start()
@@ -262,18 +265,10 @@
     def summed(pieces):
         return sum(piece[...].astype(F32) for piece in pieces)
 
-    for step in (B3, B1, B2):
-        returns[step].wait_recv()
-    whole = summed([res.at[B0], rb.at[0], rb.at[1], rb.at[2]])
-    bsum[pl.ds(0, hd), :] = whole[:hd].astype(BF16)
-    bsum[pl.ds(hd, 16), :] = split_sum(jnp.sum(whole[hd:], axis=0, keepdims=True), rows)
-    cross.start()
     own_num = [own_o[pl.ds(h * half, half), pl.ds(h * hd, hd)].T for h in range(kvh)]
-    for step in (A3, A1, A2):
-        returns[step].wait_recv()
-    near = summed([res.at[A0], ra.at[0], ra.at[1], ra.at[2]])
-    cross.wait_recv()
-    whole = near + rx[...].astype(F32)
+    for copy in arrivals.values():
+        copy.wait_recv()
+    whole = summed([res.at[A0], *(ra.at[k] for k in arrivals)])
     total = jnp.sum(whole[hd:], axis=0, keepdims=True) + own_t[pl.ds(0, 1), :]
     for h in range(kvh):
         lanes = slice(h * half, (h + 1) * half)
@@ -285,35 +280,45 @@
     local[9].wait()
     block = seqs // NZ
     width = w_v.shape[1] // CHUNKS
-    to_z, to_x = [], []
-    for k in range(CHUNKS):
+    relayed, plain, joined, to_x = {}, {}, {}, {}
+    order = [k // 2 + (k % 2) * (CHUNKS // 2) for k in range(CHUNKS)]
+    for k in order:
+        via, other = (1, 3) if k < CHUNKS // 2 else (3, 1)
         cols = pl.ds(k * width, width)
         piece = jnp.dot(att[...], w_v[:, cols], preferred_element_type=F32).astype(BF16)
         for i in range(NZ):
             pz[i, :, cols] = piece[i * block : (i + 1) * block]
-        copies = []
-        for d in (1, 3, 2):
-            n = k * 3 + d - 1
-            copies.append(
-                remote(pz.at[(z + d) % NZ, :, cols], zr.at[NZ - d - 1, :, cols], z_send.at[n], z_recv.at[n], head_at(0, d))
-            )
-            copies[-1].start()
-        to_z.append(copies)
-    for k in range(CHUNKS):
+        relayed[k] = remote(
+            pz.at[(z + 2) % NZ, :, cols], zt.at[:, cols], z_send.at[k], z_recv.at[k], head_at(0, via)
+        )
+        plain[k] = remote(
+            pz.at[(z + other) % NZ, :, cols], zr.at[other // 2, :, cols],
+            z_send.at[CHUNKS + k], z_recv.at[CHUNKS + k], head_at(0, other),
+        )
+        joined[k] = remote(
+            zj.at[:, cols], zr.at[via // 2, :, cols],
+            z_send.at[2 * CHUNKS + k], z_recv.at[2 * CHUNKS + k], head_at(0, via),
+        )
+        relayed[k].start()
+        plain[k].start()
+    for k in order:
+        via = 1 if k < CHUNKS // 2 else 3
         cols = pl.ds(k * width, width)
-        for copy in to_z[k]:
-            copy.wait_recv()
-        both = pz[z, :, cols].astype(F32)
-        for i in range(NZ - 1):
-            both = both + zr[i, :, cols].astype(F32)
+        relayed[k].wait_recv()
+        zj[:, cols] = (pz[(z + via) % NZ, :, cols].astype(F32) + zt[:, cols].astype(F32)).astype(BF16)
+        joined[k].start()
+    for k in order:
+        cols = pl.ds(k * width, width)
+        plain[k].wait_recv()
+        joined[k].wait_recv()
+        both = pz[z, :, cols].astype(F32) + zr[0, :, cols].astype(F32) + zr[1, :, cols].astype(F32)
         first, second = both[: block // 2], both[block // 2 :]
         near_sum[:, cols] = jnp.where(xl == 0, first, second)
         px[:, cols] = jnp.where(xl == 0, second, first).astype(BF16)
-        copy = remote(px.at[:, cols], xr.at[:, cols], x_send.at[k], x_recv.at[k], head_at(1, 0))
-        copy.start()
-        to_x.append(copy)
+        to_x[k] = remote(px.at[:, cols], xr.at[:, cols], x_send.at[k], x_recv.at[k], head_at(1, 0))
+        to_x[k].start()
     square = jnp.zeros((block // 2, 1), F32)
-    for k in range(CHUNKS):
+    for k in order:
         cols = pl.ds(k * width, width)
         to_x[k].wait_recv()
         projected = near_sum[:, cols] + xr[:, cols].astype(F32)
@@ -321,7 +326,7 @@
         square = square + jnp.sum(projected * projected, axis=1, keepdims=True)
     out_ref[...] = near_sum[...] / jnp.sqrt(square / w_v.shape[1] + epsilon)
 
-    for copy in (*gathers.values(), *returns.values(), cross, *sum(to_z, []), *to_x):
+    for copy in (*gathers.values(), *returns.values(), *relayed.values(), *plain.values(), *joined.values(), *to_x.values()):
         copy.wait_send()
 
 
@@ -342,8 +347,8 @@
             vmem((hot_used.shape[0] // 128, 128), I32),
             vmem((1, seqs), I32),
             pltpu.SMEM((1, seqs), I32),
-            vmem((pages, kvh, page, hd), BF16),
-            vmem((pages, kvh, page, hd), BF16),
+            vmem((pages - HOT_CAP, kvh, page, hd), BF16),
+            vmem((pages - HOT_CAP, kvh, page, hd), BF16),
             vmem((2 * HOT_CAP, kvh, page, hd), BF16),
             vmem((2 * HOT_CAP, kvh, page, hd), BF16),
             vmem((kvh, hd, 2 * HOT_CAP * page), BF16),
@@ -353,17 +358,16 @@
             vmem((8, rows), F32),
             vmem((2 * HOT_CAP, 128), F32),
             vmem((8, hd + 16, rows), BF16),
-            vmem((3, hd + 16, rows), BF16),
-            vmem((3, hd + 16, rows), BF16),
-            vmem((hd + 16, rows), BF16),
-            vmem((hd + 16, rows), BF16),
+            vmem((7, hd + 16, rows), BF16),
             vmem((page, rows), F32),
             vmem((rows, page), F32),
             vmem((rows, kvh * hd), F32),
             vmem(o_weight.shape, BF16),
             vmem((seqs, heads * hd), BF16),
             vmem((NZ, seqs // NZ, width), BF16),
-            vmem((NZ - 1, seqs // NZ, width), BF16),
+            vmem((seqs // NZ, width), BF16),
+            vmem((seqs // NZ, width), BF16),
+            vmem((2, seqs // NZ, width), BF16),
             vmem((seqs // 8, width), BF16),
             vmem((seqs // 8, width), BF16),
             vmem((seqs // 8, width), F32),
@@ -378,6 +382,7 @@
             pltpu.SemaphoreType.DMA((7,)),
             pltpu.SemaphoreType.DMA((7,)),
             pltpu.SemaphoreType.DMA((7,)),
+            pltpu.SemaphoreType.REGULAR,
         ],
         compiler_params=pltpu.CompilerParams(
             collective_id=0, has_side_effects=True, vmem_limit_bytes=66_000_000

time: 47.4 us -> 38.9 us (0.82)
  Pallas kernels: 45.6 us -> 37.1 us
    pallas_call x1, Pallas kernels: 45.6 us -> 37.1 us  [layer(): pl.pallas_call(layer_kernel, out_shape=jax.ShapeDtypeStruct((seqs // 8, w...]
where the time goes in v3:
time: 38.9 us; the launch traced here: 38.7 us
  Pallas kernels  37.1 us (95%)
  other arithmetic  1.57 us (4%)
    pallas_call x1, Pallas kernels, layer(): pl.pallas_call(layer_kernel, out_shape=jax.ShapeDtypeStruct((seqs // 8, w...  37.1 us
    convert_element_type x1, other arithmetic, per_device(): return (residual.astype(F32) + normed * norm_gain[None, :]).astype(BF16)  1.57 us

profile of v3, /device:TPU:0, one launch (start us, length us, event | category | flops | bytes accessed | tf_op | source)
XLA Modules:
  0.0 38.7 jit_solution(17861456785896516254)
XLA Ops:
  0.0 0.0 copy-start
  0.0 0.0 copy-start.1
  0.0 37.1 %layer.1 = f32[8,4608]{1,0:T(8,128)} custom-call(bf16[256,128]{1,0:T(8,128)(2,1)} %bitcast.5, bf16[72,2,128,128]{3,2,1,0:T(8,128)(2,1)} %k_hbm.1, bf16[72,2,128,128]{3,2,1,0:T(8,128)(2,1)} %v_hbm.1, s32[1,64]{1,0:T(1,128)} %bitcast.7, s32[8,128]{1,0:T(8,128)} %bitcast.6, s32[1,64]{1,0:T(1,128)} %bitcast.8, s32[1,64]{1,0:T(1,128)} %bitcast.9, ...), custom_call_target="tpu_custom_call" | custom-call | tf_op jit(solution)/shard_map/layer/pallas_call | solution.py:339
  37.1 0.0 copy-done
  37.1 0.0 copy-done.1
  37.2 1.6 %add_convert_fusion = bf16[8,4608]{1,0:T(8,128)(2,1)} fusion(f32[8,4608]{1,0:T(8,128)} %layer.1, bf16[8,4608]{1,0:T(8,128)(2,1)S(1)} %copy-done, f32[4608]{0:T(1024)S(1)} %copy-done.1), kind=kLoop, calls=%fused_computation | loop fusion | flops 147456 | bytes 313344 | tf_op jit(solution)/shard_map/convert_element_type | solution.py:407
Async XLA Ops:
  0.0 37.1 %copy-start = (bf16[8,4608]{1,0:T(8,128)(2,1)S(1)}, bf16[8,4608]{1,0:T(8,128)(2,1)}, u32[]{:S(2)}) copy-start(bf16[8,4608]{1,0:T(8,128)(2,1)} %param.18) | copy-start | bytes 221188
  0.0 37.1 %copy-start.1 = (f32[4608]{0:T(1024)S(1)}, f32[4608]{0:T(1024)}, u32[]{:S(2)}) copy-start(f32[4608]{0:T(1024)} %param.19) | copy-start | bytes 55300

commit v4 on v3

--- a/solution.py
+++ b/solution.py
@@ -18,7 +18,7 @@
 F32, BF16, I32 = jnp.float32, jnp.bfloat16, jnp.int32
 MESH = pl.DeviceIdType.MESH
 
-A3, A1, A2, B0, B3, B1, B2, A0 = range(8)
+A3, B0, A1, B3, B1, B2, A2, A0 = range(8)
 OWNER = {A3: (3, 0), A1: (1, 0), A2: (2, 0), B0: (0, 1), B3: (3, 1), B1: (1, 1), B2: (2, 1), A0: (0, 0)}
 
 
@@ -35,9 +35,9 @@
 def layer_kernel(
     q_hbm, k_hbm, v_hbm, hot_hbm, used_hbm, up_hbm, len_hbm, w_hbm, out_ref,
     q_v, hot_v, used_v, len_v, up_s, kbuf, vbuf, hk, hv, vt, qt, qbd, urow, lrow, pos,
-    res, ra, own_t, own_w, own_o,
-    w_v, att, pz, zt, zj, zr, px, xr, near_sum,
-    in_sem, z_send, z_recv, x_send, x_recv, kv_send, kv_recv, ag_send, ag_recv, rs_send, rs_recv, far_sem,
+    wt, res, ra, own_t, own_w, own_o,
+    w_v, att, pz, zt, zj, zr, near_sum,
+    in_sem, z_send, z_recv, kv_send, kv_recv, ag_send, ag_recv, rs_send, rs_recv, far_sem,
 ):
     seqs = len_v.shape[1]
     kvh, page, hd = hk.shape[1:]
@@ -106,14 +106,18 @@
         if step == A0:
             continue
         back = next(k for k, at_ in OWNER.items() if at_ == ((NY - dy) % NY, dx))
-        gathers[step] = remote(qt.at[A0], qt.at[step], ag_send.at[step], ag_recv.at[step], at((NY - dy) % NY, dx))
+        first = B0 if step in (B1, B2, B3) else A0
+        gathers[step] = remote(
+            qt.at[first], qt.at[step], ag_send.at[step], ag_recv.at[step], at((NY - dy) % NY, dx if step == B0 else 0)
+        )
         returns[step] = remote(res.at[step], ra.at[back], rs_send.at[step], rs_recv.at[back], at(dy, dx))
     arrivals = {
         step: remote(res.at[step], ra.at[step], rs_send.at[step], rs_recv.at[step], at(0, 1)) for step in returns
     }
 
-    pl.semaphore_signal(far_sem, inc=1, device_id=at(0, 1), device_id_type=MESH)
-    for step in (A3, A1, A2, B0):
+    for dz in (1, 3):
+        pl.semaphore_signal(far_sem, inc=1, device_id=head_at(0, dz), device_id_type=MESH)
+    for step in (B0, A3, A1, A2):
         gathers[step].start()
     local[5].wait()
     local[6].wait()
@@ -159,31 +163,46 @@
 
     transpose_values(0)
 
-    def shared_block(step):
-        set_queries(step)
-        allowed = jnp.where(urow[pl.ds(step, 1), :] > pos[:, pl.ds(0, 1)], 1.0, 0.0)
-        total = jnp.zeros((1, rows), F32)
+    def shared_block(step, slot, previous):
+        if step is not None:
+            set_queries(step)
+            allowed = jnp.where(urow[pl.ds(step, 1), :] > pos[:, pl.ds(0, 1)], 1.0, 0.0)
+            sums = jnp.zeros((8, rows), F32)
         parts = [jnp.zeros((hd, half), F32) for _ in range(kvh)]
-        for c in range(HOT_CAP):
+
+        def scores(c):
             keys = jnp.concatenate(
                 [hk[pl.ds(2 * c, 2), h].reshape(2 * page, hd) for h in range(kvh)], axis=1
             )
-            logits = jnp.dot(keys, qbd[0], preferred_element_type=F32)
-            weight = weights_of(logits)
-            weight = jnp.concatenate(
-                [weight[i * page : (i + 1) * page] * allowed[2 * c + i : 2 * c + i + 1] for i in range(2)], axis=0
-            )
-            total = total + jnp.sum(weight, axis=0, keepdims=True)
-            rounded = weight.astype(BF16)
+            return jnp.dot(keys, qbd[0], preferred_element_type=F32)
+
+        def values(c):
             for h in range(kvh):
                 parts[h] = parts[h] + jnp.dot(
                     vt[h, :, pl.ds(2 * c * page, 2 * page)],
-                    rounded[:, h * half : (h + 1) * half],
+                    wt[1 - slot, pl.ds(2 * c * page, 2 * page), pl.ds(h * half, half)],
                     preferred_element_type=F32,
                 )
-        for h in range(kvh):
-            res[step, pl.ds(0, hd), pl.ds(h * half, half)] = parts[h].astype(BF16)
-        res[step, pl.ds(hd, 16), :] = split_sum(total, rows)
+
+        if step is not None:
+            logits = scores(0)
+        for c in range(HOT_CAP):
+            if previous is not None:
+                values(c)
+            if step is None:
+                continue
+            for i in range(2 * page // 16):
+                j = (2 * c * page + i * 16) // page
+                weight = weights_of(logits[i * 16 : (i + 1) * 16]) * allowed[j : j + 1]
+                sums = sums + weight[:8] + weight[8:]
+                wt[slot, pl.ds(2 * c * page + i * 16, 16), :] = weight.astype(BF16)
+            if c + 1 < HOT_CAP:
+                logits = scores(c + 1)
+        if step is not None:
+            res[step, pl.ds(hd, 16), :] = split_sum(jnp.sum(sums, axis=0, keepdims=True), rows)
+        if previous is not None:
+            for h in range(kvh):
+                res[previous, pl.ds(0, hd), pl.ds(h * half, half)] = parts[h].astype(BF16)
 
     def page_of(place):
         return jnp.maximum(up_s[0, seq_at(place)] - HOT_CAP, 0)
@@ -238,28 +257,42 @@
         lax.fori_loop(0, seqs // 32, some, 0)
 
     own_scores()
-    pl.semaphore_wait(far_sem, 1)
-    for step in (B3, B1, B2):
-        gathers[step].start()
     own_weights()
     kv_copies[0].wait()
     kv_copies[1].wait()
     transpose_values(HOT_CAP)
 
-    def one_step(step, carry):
-        for k in gathers:
+    def arrive(step, steps):
+        for k in steps:
             @pl.when(step == k)
             def _():
                 gathers[k].wait_recv()
-
-        shared_block(step)
-        for k in returns:
+                if k == B0:
+                    for n in (B3, B1, B2):
+                        gathers[n].start()
+
+    def send_back(step, steps):
+        for k in steps:
             @pl.when(step == k)
             def _():
                 returns[k].start()
+
+    def two_steps(n, carry):
+        step = 2 * n + 1
+        arrive(step, (1, 3, 5))
+        shared_block(step, 1, step - 1)
+        send_back(step - 1, (0, 2, 4))
+        arrive(step + 1, (2, 4, 6))
+        shared_block(step + 1, 0, step)
+        send_back(step, (1, 3, 5))
         return carry
 
-    lax.fori_loop(0, 8, one_step, 0)
+    gathers[0].wait_recv()
+    shared_block(0, 0, None)
+    lax.fori_loop(0, 3, two_steps, 0)
+    shared_block(7, 1, 6)
+    returns[6].start()
+    shared_block(None, 0, 7)
     own_values()
 
     def summed(pieces):
@@ -280,53 +313,53 @@
     local[9].wait()
     block = seqs // NZ
     width = w_v.shape[1] // CHUNKS
-    relayed, plain, joined, to_x = {}, {}, {}, {}
+    relayed, plain, joined, across = {}, {}, {}, {}
     order = [k // 2 + (k % 2) * (CHUNKS // 2) for k in range(CHUNKS)]
+    pl.semaphore_wait(far_sem, 2)
     for k in order:
         via, other = (1, 3) if k < CHUNKS // 2 else (3, 1)
         cols = pl.ds(k * width, width)
         piece = jnp.dot(att[...], w_v[:, cols], preferred_element_type=F32).astype(BF16)
         for i in range(NZ):
-            pz[i, :, cols] = piece[i * block : (i + 1) * block]
-        relayed[k] = remote(
-            pz.at[(z + 2) % NZ, :, cols], zt.at[:, cols], z_send.at[k], z_recv.at[k], head_at(0, via)
-        )
-        plain[k] = remote(
-            pz.at[(z + other) % NZ, :, cols], zr.at[other // 2, :, cols],
-            z_send.at[CHUNKS + k], z_recv.at[CHUNKS + k], head_at(0, other),
-        )
-        joined[k] = remote(
-            zj.at[:, cols], zr.at[via // 2, :, cols],
-            z_send.at[2 * CHUNKS + k], z_recv.at[2 * CHUNKS + k], head_at(0, via),
-        )
-        relayed[k].start()
-        plain[k].start()
+            for j in range(2):
+                pz[i, j, :, cols] = piece[i * block + j * 8 : i * block + j * 8 + 8]
+
+        def to_sum(src, dx, dz, n):
+            slot = 4 if dz == 0 else 2 * dx + dz // 2
+            return remote(
+                src, zr.at[slot, :, cols], z_send.at[n * CHUNKS + k], z_recv.at[n * CHUNKS + k], head_at(dx, dz)
+            )
+
+        relayed[k] = remote(pz.at[(z + 2) % NZ, :, :, cols], zt.at[:, :, cols], z_send.at[k], z_recv.at[k], head_at(0, via))
+        plain[k] = [to_sum(pz.at[(z + other) % NZ, (xl + dx) % 2, :, cols], dx, other, 1 + dx) for dx in range(2)]
+        joined[k] = [to_sum(zj.at[(xl + dx) % 2, :, cols], dx, via, 3 + dx) for dx in range(2)]
+        across[k] = [to_sum(pz.at[z, 1 - xl, :, cols], 1, 0, 5)]
+        for copy in (relayed[k], *plain[k], *across[k]):
+            copy.start()
     for k in order:
         via = 1 if k < CHUNKS // 2 else 3
         cols = pl.ds(k * width, width)
         relayed[k].wait_recv()
-        zj[:, cols] = (pz[(z + via) % NZ, :, cols].astype(F32) + zt[:, cols].astype(F32)).astype(BF16)
-        joined[k].start()
-    for k in order:
-        cols = pl.ds(k * width, width)
-        plain[k].wait_recv()
-        joined[k].wait_recv()
-        both = pz[z, :, cols].astype(F32) + zr[0, :, cols].astype(F32) + zr[1, :, cols].astype(F32)
-        first, second = both[: block // 2], both[block // 2 :]
-        near_sum[:, cols] = jnp.where(xl == 0, first, second)
-        px[:, cols] = jnp.where(xl == 0, second, first).astype(BF16)
-        to_x[k] = remote(px.at[:, cols], xr.at[:, cols], x_send.at[k], x_recv.at[k], head_at(1, 0))
-        to_x[k].start()
+        for j in range(2):
+            zj[j, :, cols] = (pz[(z + via) % NZ, j, :, cols].astype(F32) + zt[j, :, cols].astype(F32)).astype(BF16)
+        for copy in joined[k]:
+            copy.start()
     square = jnp.zeros((block // 2, 1), F32)
     for k in order:
         cols = pl.ds(k * width, width)
-        to_x[k].wait_recv()
-        projected = near_sum[:, cols] + xr[:, cols].astype(F32)
+        for copy in (*plain[k], *across[k]):
+            copy.wait_recv()
+        for copy in joined[k]:
+            copy.wait_recv()
+        projected = pz[z, xl, :, cols].astype(F32)
+        for i in range(5):
+            projected = projected + zr[i, :, cols].astype(F32)
         near_sum[:, cols] = projected
         square = square + jnp.sum(projected * projected, axis=1, keepdims=True)
     out_ref[...] = near_sum[...] / jnp.sqrt(square / w_v.shape[1] + epsilon)
 
-    for copy in (*gathers.values(), *returns.values(), *relayed.values(), *plain.values(), *joined.values(), *to_x.values()):
+    sent = [*gathers.values(), *returns.values(), *relayed.values()]
+    for copy in sum([*plain.values(), *joined.values(), *across.values()], sent):
         copy.wait_send()
 
 
@@ -357,6 +390,7 @@
             vmem((8, rows), F32),
             vmem((8, rows), F32),
             vmem((2 * HOT_CAP, 128), F32),
+            vmem((2, 2 * HOT_CAP * page, rows), BF16),
             vmem((8, hd + 16, rows), BF16),
             vmem((7, hd + 16, rows), BF16),
             vmem((page, rows), F32),
@@ -364,18 +398,14 @@
             vmem((rows, kvh * hd), F32),
             vmem(o_weight.shape, BF16),
             vmem((seqs, heads * hd), BF16),
-            vmem((NZ, seqs // NZ, width), BF16),
-            vmem((seqs // NZ, width), BF16),
-            vmem((seqs // NZ, width), BF16),
-            vmem((2, seqs // NZ, width), BF16),
-            vmem((seqs // 8, width), BF16),
-            vmem((seqs // 8, width), BF16),
+            vmem((NZ, 2, 8, width), BF16),
+            vmem((2, 8, width), BF16),
+            vmem((2, 8, width), BF16),
+            vmem((5, 8, width), BF16),
             vmem((seqs // 8, width), F32),
             pltpu.SemaphoreType.DMA((10,)),
-            pltpu.SemaphoreType.DMA((3 * CHUNKS,)),
-            pltpu.SemaphoreType.DMA((3 * CHUNKS,)),
-            pltpu.SemaphoreType.DMA((CHUNKS,)),
-            pltpu.SemaphoreType.DMA((CHUNKS,)),
+            pltpu.SemaphoreType.DMA((6 * CHUNKS,)),
+            pltpu.SemaphoreType.DMA((6 * CHUNKS,)),
             pltpu.SemaphoreType.DMA((2,)),
             pltpu.SemaphoreType.DMA((2,)),
             pltpu.SemaphoreType.DMA((7,)),
@@ -385,7 +415,7 @@
             pltpu.SemaphoreType.REGULAR,
         ],
         compiler_params=pltpu.CompilerParams(
-            collective_id=0, has_side_effects=True, vmem_limit_bytes=66_000_000
+            collective_id=0, has_side_effects=True, vmem_limit_bytes=64_500_000
         ),
         name="layer",
     )(

time: 38.9 us -> 36.5 us (0.938)
  Pallas kernels: 37.1 us -> 34.8 us
    pallas_call x1, Pallas kernels: 37.1 us -> 34.8 us  [layer(): pl.pallas_call(layer_kernel, out_shape=jax.ShapeDtypeStruct((seqs // 8, w...]
where the time goes in v4:
time: 36.5 us; the launch traced here: 36.4 us
  Pallas kernels  34.8 us (95%)
  other arithmetic  1.57 us (4%)
    pallas_call x1, Pallas kernels, layer(): pl.pallas_call(layer_kernel, out_shape=jax.ShapeDtypeStruct((seqs // 8, w...  34.8 us
    convert_element_type x1, other arithmetic, per_device(): return (residual.astype(F32) + normed * norm_gain[None, :]).astype(BF16)  1.57 us

profile of v4, /device:TPU:0, one launch (start us, length us, event | category | flops | bytes accessed | tf_op | source)
XLA Modules:
  0.0 36.4 jit_solution(12373347830548804376)
XLA Ops:
  0.0 0.0 copy-start
  0.0 0.0 copy-start.1
  0.0 34.8 %layer.1 = f32[8,4608]{1,0:T(8,128)} custom-call(bf16[256,128]{1,0:T(8,128)(2,1)} %bitcast.5, bf16[72,2,128,128]{3,2,1,0:T(8,128)(2,1)} %k_hbm.1, bf16[72,2,128,128]{3,2,1,0:T(8,128)(2,1)} %v_hbm.1, s32[1,64]{1,0:T(1,128)} %bitcast.7, s32[8,128]{1,0:T(8,128)} %bitcast.6, s32[1,64]{1,0:T(1,128)} %bitcast.8, s32[1,64]{1,0:T(1,128)} %bitcast.9, ...), custom_call_target="tpu_custom_call" | custom-call | tf_op jit(solution)/shard_map/layer/pallas_call | solution.py:372
  34.8 0.0 copy-done
  34.8 0.0 copy-done.1
  34.8 1.6 %add_convert_fusion = bf16[8,4608]{1,0:T(8,128)(2,1)} fusion(f32[8,4608]{1,0:T(8,128)} %layer.1, bf16[8,4608]{1,0:T(8,128)(2,1)S(1)} %copy-done, f32[4608]{0:T(1024)S(1)} %copy-done.1), kind=kLoop, calls=%fused_computation | loop fusion | flops 147456 | bytes 313344 | tf_op jit(solution)/shard_map/convert_element_type | solution.py:437
Async XLA Ops:
  0.0 34.8 %copy-start = (bf16[8,4608]{1,0:T(8,128)(2,1)S(1)}, bf16[8,4608]{1,0:T(8,128)(2,1)}, u32[]{:S(2)}) copy-start(bf16[8,4608]{1,0:T(8,128)(2,1)} %param.18) | copy-start | bytes 221188
  0.0 34.8 %copy-start.1 = (f32[4608]{0:T(1024)S(1)}, f32[4608]{0:T(1024)}, u32[]{:S(2)}) copy-start(f32[4608]{0:T(1024)} %param.19) | copy-start | bytes 55300

commit v5 on v4

--- a/solution.py
+++ b/solution.py
@@ -14,11 +14,11 @@
 epsilon = 1e-06
 NY = 4
 NZ = 4
-CHUNKS = 4
+CHUNKS = 6
 F32, BF16, I32 = jnp.float32, jnp.bfloat16, jnp.int32
 MESH = pl.DeviceIdType.MESH
 
-A3, B0, A1, B3, B1, B2, A2, A0 = range(8)
+A3, B0, A1, B3, A2, B1, B2, A0 = range(8)
 OWNER = {A3: (3, 0), A1: (1, 0), A2: (2, 0), B0: (0, 1), B3: (3, 1), B1: (1, 1), B2: (2, 1), A0: (0, 0)}
 
 
@@ -37,7 +37,7 @@
     q_v, hot_v, used_v, len_v, up_s, kbuf, vbuf, hk, hv, vt, qt, qbd, urow, lrow, pos,
     wt, res, ra, own_t, own_w, own_o,
     w_v, att, pz, zt, zj, zr, near_sum,
-    in_sem, z_send, z_recv, kv_send, kv_recv, ag_send, ag_recv, rs_send, rs_recv, far_sem,
+    in_sem, z_send, z_recv, kv_send, kv_recv, ag_send, ag_recv, rs_send, rs_recv, far_sem, diag_sem,
 ):
     seqs = len_v.shape[1]
     kvh, page, hd = hk.shape[1:]
@@ -106,17 +106,15 @@
         if step == A0:
             continue
         back = next(k for k, at_ in OWNER.items() if at_ == ((NY - dy) % NY, dx))
-        first = B0 if step in (B1, B2, B3) else A0
-        gathers[step] = remote(
-            qt.at[first], qt.at[step], ag_send.at[step], ag_recv.at[step], at((NY - dy) % NY, dx if step == B0 else 0)
-        )
+        gathers[step] = remote(qt.at[A0], qt.at[step], ag_send.at[step], ag_recv.at[step], at((NY - dy) % NY, dx))
         returns[step] = remote(res.at[step], ra.at[back], rs_send.at[step], rs_recv.at[back], at(dy, dx))
     arrivals = {
         step: remote(res.at[step], ra.at[step], rs_send.at[step], rs_recv.at[step], at(0, 1)) for step in returns
     }
 
+    pl.semaphore_signal(far_sem, inc=1, device_id=at(0, 1), device_id_type=MESH)
     for dz in (1, 3):
-        pl.semaphore_signal(far_sem, inc=1, device_id=head_at(0, dz), device_id_type=MESH)
+        pl.semaphore_signal(diag_sem, inc=1, device_id=head_at(0, dz), device_id_type=MESH)
     for step in (B0, A3, A1, A2):
         gathers[step].start()
     local[5].wait()
@@ -207,10 +205,7 @@
     def page_of(place):
         return jnp.maximum(up_s[0, seq_at(place)] - HOT_CAP, 0)
 
-    def own_scores():
-        local[7].wait()
-        set_queries(A0)
-
+    def own_scores(first, last):
         def some(g, carry):
             seq_of = lax.broadcasted_iota(I32, (page, rows), 1) % seqs
             tile = own_t[...]
@@ -225,8 +220,7 @@
             own_t[...] = tile
             return carry
 
-        own_t[...] = jnp.zeros_like(own_t)
-        lax.fori_loop(0, seqs // 16, some, 0)
+        lax.fori_loop(first, last, some, 0)
 
     def own_weights():
         token = lax.broadcasted_iota(I32, (page, rows), 0).astype(F32)
@@ -256,8 +250,13 @@
 
         lax.fori_loop(0, seqs // 32, some, 0)
 
-    own_scores()
-    own_weights()
+    set_queries(A0)
+    own_t[...] = jnp.zeros_like(own_t)
+    local[7].wait()
+    own_scores(0, seqs // 32)
+    pl.semaphore_wait(far_sem, 1)
+    for step in (B3, B1, B2):
+        gathers[step].start()
     kv_copies[0].wait()
     kv_copies[1].wait()
     transpose_values(HOT_CAP)
@@ -267,9 +266,6 @@
             @pl.when(step == k)
             def _():
                 gathers[k].wait_recv()
-                if k == B0:
-                    for n in (B3, B1, B2):
-                        gathers[n].start()
 
     def send_back(step, steps):
         for k in steps:
@@ -293,6 +289,8 @@
     shared_block(7, 1, 6)
     returns[6].start()
     shared_block(None, 0, 7)
+    own_scores(seqs // 32, seqs // 16)
+    own_weights()
     own_values()
 
     def summed(pieces):
@@ -315,7 +313,7 @@
     width = w_v.shape[1] // CHUNKS
     relayed, plain, joined, across = {}, {}, {}, {}
     order = [k // 2 + (k % 2) * (CHUNKS // 2) for k in range(CHUNKS)]
-    pl.semaphore_wait(far_sem, 2)
+    pl.semaphore_wait(diag_sem, 2)
     for k in order:
         via, other = (1, 3) if k < CHUNKS // 2 else (3, 1)
         cols = pl.ds(k * width, width)
@@ -334,7 +332,9 @@
         plain[k] = [to_sum(pz.at[(z + other) % NZ, (xl + dx) % 2, :, cols], dx, other, 1 + dx) for dx in range(2)]
         joined[k] = [to_sum(zj.at[(xl + dx) % 2, :, cols], dx, via, 3 + dx) for dx in range(2)]
         across[k] = [to_sum(pz.at[z, 1 - xl, :, cols], 1, 0, 5)]
-        for copy in (relayed[k], *plain[k], *across[k]):
+        relayed[k].start()
+    for k in order:
+        for copy in (*plain[k], *across[k]):
             copy.start()
     for k in order:
         via = 1 if k < CHUNKS // 2 else 3
@@ -371,7 +371,7 @@
     vmem = pltpu.VMEM
     return pl.pallas_call(
         layer_kernel,
-        out_shape=jax.ShapeDtypeStruct((seqs // 8, width), F32),
+        out_shape=pltpu.VMEM((seqs // 8, width), F32),
         in_specs=[pl.BlockSpec(memory_space=pl.ANY)] * 8,
         out_specs=pl.BlockSpec(memory_space=pltpu.VMEM),
         scratch_shapes=[
@@ -413,6 +413,7 @@
             pltpu.SemaphoreType.DMA((7,)),
             pltpu.SemaphoreType.DMA((7,)),
             pltpu.SemaphoreType.REGULAR,
+            pltpu.SemaphoreType.REGULAR,
         ],
         compiler_params=pltpu.CompilerParams(
             collective_id=0, has_side_effects=True, vmem_limit_bytes=64_500_000

time: 36.5 us -> 33.6 us (0.921)
  Pallas kernels: 34.8 us -> 32.8 us
  other arithmetic: 1.57 us -> 0.66 us
    pallas_call x1, Pallas kernels: 34.8 us -> 32.8 us  [layer(): pl.pallas_call(layer_kernel, out_shape=pltpu.VMEM((seqs // 8, width), F32...]
    convert_element_type x1, other arithmetic: 1.57 us -> 0.66 us  [per_device(): return (residual.astype(F32) + normed * norm_gain[None, :]).astype(BF16)]
where the time goes in v5:
time: 33.6 us; the launch traced here: 33.5 us
  Pallas kernels  32.8 us (98%)
  other arithmetic  0.66 us (2%)
    pallas_call x1, Pallas kernels, layer(): pl.pallas_call(layer_kernel, out_shape=pltpu.VMEM((seqs // 8, width), F32...  32.8 us

profile of v5, /device:TPU:0, one launch (start us, length us, event | category | flops | bytes accessed | tf_op | source)
XLA Modules:
  0.0 33.5 jit_solution(10631615836657383534)
XLA Ops:
  0.0 0.0 copy-start
  0.0 0.0 copy-start.1
  0.0 32.8 %layer.1 = f32[8,4608]{1,0:T(8,128)S(1)} custom-call(bf16[256,128]{1,0:T(8,128)(2,1)} %bitcast.5, bf16[72,2,128,128]{3,2,1,0:T(8,128)(2,1)} %k_hbm.1, bf16[72,2,128,128]{3,2,1,0:T(8,128)(2,1)} %v_hbm.1, s32[1,64]{1,0:T(1,128)} %bitcast.7, s32[8,128]{1,0:T(8,128)} %bitcast.6, s32[1,64]{1,0:T(1,128)} %bitcast.8, s32[1,64]{1,0:T(1,128)} %bitcast.9, ...), custom_call_target="tpu_custom_call" | custom-call | tf_op jit(solution)/shard_map/layer/pallas_call | solution.py:372
  32.8 0.0 copy-done
  32.8 0.0 copy-done.1
  32.9 0.7 %add_convert_fusion = bf16[8,4608]{1,0:T(8,128)(2,1)} fusion(f32[8,4608]{1,0:T(8,128)S(1)} %layer.1, bf16[8,4608]{1,0:T(8,128)(2,1)S(1)} %copy-done, f32[4608]{0:T(1024)S(1)} %copy-done.1), kind=kLoop, calls=%fused_computation | loop fusion | flops 147456 | bytes 313344 | tf_op jit(solution)/shard_map/convert_element_type | solution.py:438
Async XLA Ops:
  0.0 32.8 %copy-start = (bf16[8,4608]{1,0:T(8,128)(2,1)S(1)}, bf16[8,4608]{1,0:T(8,128)(2,1)}, u32[]{:S(2)}) copy-start(bf16[8,4608]{1,0:T(8,128)(2,1)} %param.18) | copy-start | bytes 221188
  0.0 32.8 %copy-start.1 = (f32[4608]{0:T(1024)S(1)}, f32[4608]{0:T(1024)}, u32[]{:S(2)}) copy-start(f32[4608]{0:T(1024)} %param.19) | copy-start | bytes 55300

commit v6 on v5

--- a/solution.py
+++ b/solution.py
@@ -65,6 +65,9 @@
 
     own = pl.ds(HOT_CAP, k_hbm.shape[0] - HOT_CAP)
     hot = pl.ds(0, HOT_CAP)
+    def settle(like, semaphore):
+        pltpu.make_async_copy(like, like, semaphore).wait()
+
     local = [
         pltpu.make_async_copy(q_hbm, q_v, in_sem.at[0]),
         pltpu.make_async_copy(hot_hbm, hot_v, in_sem.at[1]),
@@ -98,18 +101,18 @@
 
     far = pl.ds(HOT_CAP, HOT_CAP)
     kv_copies = [
-        remote(hk.at[hot], hk.at[far], kv_send.at[0], kv_recv.at[0], at(0, 0, 1)),
-        remote(hv.at[hot], hv.at[far], kv_send.at[1], kv_recv.at[1], at(0, 0, 1)),
+        remote(hk.at[hot], hk.at[far], kv_send, kv_recv.at[0], at(0, 0, 1)),
+        remote(hv.at[hot], hv.at[far], kv_send, kv_recv.at[1], at(0, 0, 1)),
     ]
     gathers, returns = {}, {}
     for step, (dy, dx) in OWNER.items():
         if step == A0:
             continue
         back = next(k for k, at_ in OWNER.items() if at_ == ((NY - dy) % NY, dx))
-        gathers[step] = remote(qt.at[A0], qt.at[step], ag_send.at[step], ag_recv.at[step], at((NY - dy) % NY, dx))
-        returns[step] = remote(res.at[step], ra.at[back], rs_send.at[step], rs_recv.at[back], at(dy, dx))
+        gathers[step] = remote(qt.at[A0], qt.at[step], ag_send, ag_recv.at[step], at((NY - dy) % NY, dx))
+        returns[step] = remote(res.at[step], ra.at[back], rs_send, rs_recv.at[back], at(dy, dx))
     arrivals = {
-        step: remote(res.at[step], ra.at[step], rs_send.at[step], rs_recv.at[step], at(0, 1)) for step in returns
+        step: remote(res.at[step], ra.at[step], rs_send, rs_recv.at[step], at(0, 1)) for step in returns
     }
 
     pl.semaphore_signal(far_sem, inc=1, device_id=at(0, 1), device_id_type=MESH)
@@ -257,9 +260,7 @@
     pl.semaphore_wait(far_sem, 1)
     for step in (B3, B1, B2):
         gathers[step].start()
-    kv_copies[0].wait()
-    kv_copies[1].wait()
-    transpose_values(HOT_CAP)
+    kv_copies[0].wait_recv()
 
     def arrive(step, steps):
         for k in steps:
@@ -285,9 +286,12 @@
 
     gathers[0].wait_recv()
     shared_block(0, 0, None)
+    kv_copies[1].wait_recv()
+    transpose_values(HOT_CAP)
     lax.fori_loop(0, 3, two_steps, 0)
-    shared_block(7, 1, 6)
+    shared_block(None, 1, 6)
     returns[6].start()
+    shared_block(7, 1, None)
     shared_block(None, 0, 7)
     own_scores(seqs // 32, seqs // 16)
     own_weights()
@@ -314,24 +318,27 @@
     relayed, plain, joined, across = {}, {}, {}, {}
     order = [k // 2 + (k % 2) * (CHUNKS // 2) for k in range(CHUNKS)]
     pl.semaphore_wait(diag_sem, 2)
-    for k in order:
+    def piece_of(k):
+        return jnp.dot(att[...], w_v[:, pl.ds(k * width, width)], preferred_element_type=F32).astype(BF16)
+
+    piece = piece_of(order[0])
+    for n, k in enumerate(order):
         via, other = (1, 3) if k < CHUNKS // 2 else (3, 1)
         cols = pl.ds(k * width, width)
-        piece = jnp.dot(att[...], w_v[:, cols], preferred_element_type=F32).astype(BF16)
+        later = piece_of(order[n + 1]) if n + 1 < CHUNKS else None
         for i in range(NZ):
             for j in range(2):
                 pz[i, j, :, cols] = piece[i * block + j * 8 : i * block + j * 8 + 8]
+        piece = later
 
         def to_sum(src, dx, dz, n):
             slot = 4 if dz == 0 else 2 * dx + dz // 2
-            return remote(
-                src, zr.at[slot, :, cols], z_send.at[n * CHUNKS + k], z_recv.at[n * CHUNKS + k], head_at(dx, dz)
-            )
-
-        relayed[k] = remote(pz.at[(z + 2) % NZ, :, :, cols], zt.at[:, :, cols], z_send.at[k], z_recv.at[k], head_at(0, via))
-        plain[k] = [to_sum(pz.at[(z + other) % NZ, (xl + dx) % 2, :, cols], dx, other, 1 + dx) for dx in range(2)]
-        joined[k] = [to_sum(zj.at[(xl + dx) % 2, :, cols], dx, via, 3 + dx) for dx in range(2)]
-        across[k] = [to_sum(pz.at[z, 1 - xl, :, cols], 1, 0, 5)]
+            return remote(src, zr.at[slot, :, cols], z_send.at[n], z_recv.at[CHUNKS + k], head_at(dx, dz))
+
+        relayed[k] = remote(pz.at[(z + 2) % NZ, :, :, cols], zt.at[:, :, cols], z_send.at[0], z_recv.at[k], head_at(0, via))
+        plain[k] = [to_sum(pz.at[(z + other) % NZ, (xl + dx) % 2, :, cols], dx, other, 1) for dx in range(2)]
+        joined[k] = [to_sum(zj.at[(xl + dx) % 2, :, cols], dx, via, 2) for dx in range(2)]
+        across[k] = [to_sum(pz.at[z, 1 - xl, :, cols], 1, 0, 3)]
         relayed[k].start()
     for k in order:
         for copy in (*plain[k], *across[k]):
@@ -347,10 +354,7 @@
     square = jnp.zeros((block // 2, 1), F32)
     for k in order:
         cols = pl.ds(k * width, width)
-        for copy in (*plain[k], *across[k]):
-            copy.wait_recv()
-        for copy in joined[k]:
-            copy.wait_recv()
+        settle(zr.at[:, :, cols], z_recv.at[CHUNKS + k])
         projected = pz[z, xl, :, cols].astype(F32)
         for i in range(5):
             projected = projected + zr[i, :, cols].astype(F32)
@@ -358,9 +362,12 @@
         square = square + jnp.sum(projected * projected, axis=1, keepdims=True)
     out_ref[...] = near_sum[...] / jnp.sqrt(square / w_v.shape[1] + epsilon)
 
-    sent = [*gathers.values(), *returns.values(), *relayed.values()]
-    for copy in sum([*plain.values(), *joined.values(), *across.values()], sent):
-        copy.wait_send()
+    settle(hk.at[pl.ds(0, 2 * HOT_CAP)], kv_send)
+    settle(qt.at[pl.ds(0, len(gathers))], ag_send)
+    settle(ra, rs_send)
+    for n in range(3):
+        settle(zt, z_send.at[n])
+    settle(zr.at[0], z_send.at[3])
 
 
 def layer(queries, keys, values, hot_pages, hot_used, user_pages, lengths, o_weight):
@@ -404,13 +411,13 @@
             vmem((5, 8, width), BF16),
             vmem((seqs // 8, width), F32),
             pltpu.SemaphoreType.DMA((10,)),
-            pltpu.SemaphoreType.DMA((6 * CHUNKS,)),
-            pltpu.SemaphoreType.DMA((6 * CHUNKS,)),
+            pltpu.SemaphoreType.DMA((4,)),
+            pltpu.SemaphoreType.DMA((2 * CHUNKS,)),
+            pltpu.SemaphoreType.DMA,
             pltpu.SemaphoreType.DMA((2,)),
-            pltpu.SemaphoreType.DMA((2,)),
+            pltpu.SemaphoreType.DMA,
             pltpu.SemaphoreType.DMA((7,)),
-            pltpu.SemaphoreType.DMA((7,)),
-            pltpu.SemaphoreType.DMA((7,)),
+            pltpu.SemaphoreType.DMA,
             pltpu.SemaphoreType.DMA((7,)),
             pltpu.SemaphoreType.REGULAR,
             pltpu.SemaphoreType.REGULAR,

time: 33.6 us -> 32.8 us (0.976)
  Pallas kernels: 32.8 us -> 31.9 us
    pallas_call x1, Pallas kernels: 32.8 us -> 31.9 us  [layer(): pl.pallas_call(layer_kernel, out_shape=pltpu.VMEM((seqs // 8, width), F32...]
where the time goes in v6:
time: 32.8 us; the launch traced here: 32.6 us
  Pallas kernels  31.9 us (97%)
  other arithmetic  0.66 us (2%)
    pallas_call x1, Pallas kernels, layer(): pl.pallas_call(layer_kernel, out_shape=pltpu.VMEM((seqs // 8, width), F32...  31.9 us
    convert_element_type x1, other arithmetic, per_device(): return (residual.astype(F32) + normed * norm_gain[None, :]).astype(BF16)  0.66 us

profile of v6, /device:TPU:0, one launch (start us, length us, event | category | flops | bytes accessed | tf_op | source)
XLA Modules:
  0.0 32.6 jit_solution(12724503106839030171)
XLA Ops:
  0.0 0.0 copy-start
  0.0 0.0 copy-start.1
  0.0 31.9 %layer.1 = f32[8,4608]{1,0:T(8,128)S(1)} custom-call(bf16[256,128]{1,0:T(8,128)(2,1)} %bitcast.5, bf16[72,2,128,128]{3,2,1,0:T(8,128)(2,1)} %k_hbm.1, bf16[72,2,128,128]{3,2,1,0:T(8,128)(2,1)} %v_hbm.1, s32[1,64]{1,0:T(1,128)} %bitcast.7, s32[8,128]{1,0:T(8,128)} %bitcast.6, s32[1,64]{1,0:T(1,128)} %bitcast.8, s32[1,64]{1,0:T(1,128)} %bitcast.9, ...), custom_call_target="tpu_custom_call" | custom-call | tf_op jit(solution)/shard_map/layer/pallas_call | solution.py:379
  31.9 0.0 copy-done
  31.9 0.0 copy-done.1
  31.9 0.7 %add_convert_fusion = bf16[8,4608]{1,0:T(8,128)(2,1)} fusion(f32[8,4608]{1,0:T(8,128)S(1)} %layer.1, bf16[8,4608]{1,0:T(8,128)(2,1)S(1)} %copy-done, f32[4608]{0:T(1024)S(1)} %copy-done.1), kind=kLoop, calls=%fused_computation | loop fusion | flops 147456 | bytes 313344 | tf_op jit(solution)/shard_map/convert_element_type | solution.py:445
Async XLA Ops:
  0.0 31.9 %copy-start = (bf16[8,4608]{1,0:T(8,128)(2,1)S(1)}, bf16[8,4608]{1,0:T(8,128)(2,1)}, u32[]{:S(2)}) copy-start(bf16[8,4608]{1,0:T(8,128)(2,1)} %param.18) | copy-start | bytes 221188
  0.0 31.9 %copy-start.1 = (f32[4608]{0:T(1024)S(1)}, f32[4608]{0:T(1024)}, u32[]{:S(2)}) copy-start(f32[4608]{0:T(1024)} %param.19) | copy-start | bytes 55300

commit v7 on v6

--- a/solution.py
+++ b/solution.py
@@ -18,7 +18,7 @@
 F32, BF16, I32 = jnp.float32, jnp.bfloat16, jnp.int32
 MESH = pl.DeviceIdType.MESH
 
-A3, B0, A1, B3, A2, B1, B2, A0 = range(8)
+A3, B0, A1, A2, B2, B1, B3, A0 = range(8)
 OWNER = {A3: (3, 0), A1: (1, 0), A2: (2, 0), B0: (0, 1), B3: (3, 1), B1: (1, 1), B2: (2, 1), A0: (0, 0)}
 
 
@@ -89,11 +89,11 @@
     for peer in peers:
         pl.semaphore_signal(barrier, inc=1, device_id=peer, device_id_type=MESH)
 
-    local[0].wait()
     r = lax.broadcasted_iota(I32, (rows, rows), 0)
     col = lax.broadcasted_iota(I32, (rows, rows), 1)
     heads = rows // seqs
     perm = jnp.where(col == seq_at(r % seqs) * heads + r // seqs, 1.0, 0.0).astype(BF16)
+    local[0].wait()
     q_rows = jnp.dot(perm, q_v[...], preferred_element_type=F32)
     qt[A0] = q_rows.T.astype(BF16)
 
@@ -110,11 +110,7 @@
             continue
         back = next(k for k, at_ in OWNER.items() if at_ == ((NY - dy) % NY, dx))
         gathers[step] = remote(qt.at[A0], qt.at[step], ag_send, ag_recv.at[step], at((NY - dy) % NY, dx))
-        returns[step] = remote(res.at[step], ra.at[back], rs_send, rs_recv.at[back], at(dy, dx))
-    arrivals = {
-        step: remote(res.at[step], ra.at[step], rs_send, rs_recv.at[step], at(0, 1)) for step in returns
-    }
-
+        returns[step] = remote(res.at[step], ra.at[back], rs_send, rs_recv, at(dy, dx))
     pl.semaphore_signal(far_sem, inc=1, device_id=at(0, 1), device_id_type=MESH)
     for dz in (1, 3):
         pl.semaphore_signal(diag_sem, inc=1, device_id=head_at(0, dz), device_id_type=MESH)
@@ -122,8 +118,7 @@
         gathers[step].start()
     local[5].wait()
     local[6].wait()
-    for copy in kv_copies:
-        copy.start()
+    kv_copies[0].start()
     local[8].start()
     local[9].start()
 
@@ -258,8 +253,9 @@
     local[7].wait()
     own_scores(0, seqs // 32)
     pl.semaphore_wait(far_sem, 1)
-    for step in (B3, B1, B2):
+    for step in (B2, B1, B3):
         gathers[step].start()
+    kv_copies[1].start()
     kv_copies[0].wait_recv()
 
     def arrive(step, steps):
@@ -301,9 +297,8 @@
         return sum(piece[...].astype(F32) for piece in pieces)
 
     own_num = [own_o[pl.ds(h * half, half), pl.ds(h * hd, hd)].T for h in range(kvh)]
-    for copy in arrivals.values():
-        copy.wait_recv()
-    whole = summed([res.at[A0], *(ra.at[k] for k in arrivals)])
+    settle(ra, rs_recv)
+    whole = summed([res.at[A0], *(ra.at[k] for k in returns)])
     total = jnp.sum(whole[hd:], axis=0, keepdims=True) + own_t[pl.ds(0, 1), :]
     for h in range(kvh):
         lanes = slice(h * half, (h + 1) * half)
@@ -418,7 +413,7 @@
             pltpu.SemaphoreType.DMA,
             pltpu.SemaphoreType.DMA((7,)),
             pltpu.SemaphoreType.DMA,
-            pltpu.SemaphoreType.DMA((7,)),
+            pltpu.SemaphoreType.DMA,
             pltpu.SemaphoreType.REGULAR,
             pltpu.SemaphoreType.REGULAR,
         ],

time: 32.8 us -> 32.3 us (0.985)
  Pallas kernels: 31.9 us -> 31.5 us
    pallas_call x1, Pallas kernels: 31.9 us -> 31.5 us  [layer(): pl.pallas_call(layer_kernel, out_shape=pltpu.VMEM((seqs // 8, width), F32...]
where the time goes in v7:
time: 32.3 us; the launch traced here: 32.2 us
  Pallas kernels  31.5 us (98%)
  other arithmetic  0.66 us (2%)
    pallas_call x1, Pallas kernels, layer(): pl.pallas_call(layer_kernel, out_shape=pltpu.VMEM((seqs // 8, width), F32...  31.5 us
    convert_element_type x1, other arithmetic, per_device(): return (residual.astype(F32) + normed * norm_gain[None, :]).astype(BF16)  0.66 us

profile of v7, /device:TPU:0, one launch (start us, length us, event | category | flops | bytes accessed | tf_op | source)
XLA Modules:
  0.0 32.2 jit_solution(17634318751388010114)
XLA Ops:
  0.0 0.0 copy-start
  0.0 0.0 copy-start.1
  0.0 31.5 %layer.1 = f32[8,4608]{1,0:T(8,128)S(1)} custom-call(bf16[256,128]{1,0:T(8,128)(2,1)} %bitcast.5, bf16[72,2,128,128]{3,2,1,0:T(8,128)(2,1)} %k_hbm.1, bf16[72,2,128,128]{3,2,1,0:T(8,128)(2,1)} %v_hbm.1, s32[1,64]{1,0:T(1,128)} %bitcast.7, s32[8,128]{1,0:T(8,128)} %bitcast.6, s32[1,64]{1,0:T(1,128)} %bitcast.8, s32[1,64]{1,0:T(1,128)} %bitcast.9, ...), custom_call_target="tpu_custom_call" | custom-call | tf_op jit(solution)/shard_map/layer/pallas_call | solution.py:374
  31.5 0.0 copy-done
  31.5 0.0 copy-done.1
  31.5 0.7 %add_convert_fusion = bf16[8,4608]{1,0:T(8,128)(2,1)} fusion(f32[8,4608]{1,0:T(8,128)S(1)} %layer.1, bf16[8,4608]{1,0:T(8,128)(2,1)S(1)} %copy-done, f32[4608]{0:T(1024)S(1)} %copy-done.1), kind=kLoop, calls=%fused_computation | loop fusion | flops 147456 | bytes 313344 | tf_op jit(solution)/shard_map/convert_element_type | solution.py:440
Async XLA Ops:
  0.0 31.5 %copy-start = (bf16[8,4608]{1,0:T(8,128)(2,1)S(1)}, bf16[8,4608]{1,0:T(8,128)(2,1)}, u32[]{:S(2)}) copy-start(bf16[8,4608]{1,0:T(8,128)(2,1)} %param.18) | copy-start | bytes 221188
  0.0 31.5 %copy-start.1 = (f32[4608]{0:T(1024)S(1)}, f32[4608]{0:T(1024)}, u32[]{:S(2)}) copy-start(f32[4608]{0:T(1024)} %param.19) | copy-start | bytes 55300

commit v8 on v7

--- a/solution.py
+++ b/solution.py
@@ -26,18 +26,12 @@
     return jnp.exp2(jnp.tanh(logits * (score_scale / soft_cap)) * (soft_cap * math.log2(math.e)))
 
 
-def split_sum(totals, rows):
-    high = totals.astype(BF16).astype(F32)
-    row = lax.broadcasted_iota(I32, (16, rows), 0)
-    return jnp.where(row == 0, high, jnp.where(row == 1, totals - high, 0.0)).astype(BF16)
-
-
 def layer_kernel(
     q_hbm, k_hbm, v_hbm, hot_hbm, used_hbm, up_hbm, len_hbm, w_hbm, out_ref,
     q_v, hot_v, used_v, len_v, up_s, kbuf, vbuf, hk, hv, vt, qt, qbd, urow, lrow, pos,
-    wt, res, ra, own_t, own_w, own_o,
+    wt, res, ra, tot, tot_ra, own_t, own_w, own_o,
     w_v, att, pz, zt, zj, zr, near_sum,
-    in_sem, z_send, z_recv, kv_send, kv_recv, ag_send, ag_recv, rs_send, rs_recv, far_sem, diag_sem,
+    in_sem, z_send, z_recv, kv_send, kv_recv, ag_send, ag_recv, rs_send, rs_recv, tot_send, tot_recv, far_sem, diag_sem,
 ):
     seqs = len_v.shape[1]
     kvh, page, hd = hk.shape[1:]
@@ -85,7 +79,7 @@
 
     barrier = pltpu.get_barrier_semaphore()
     peers = [at(1), at(2), at(3), at(0, 1), at(0, 0, 1)]
-    peers += [head_at(0, 1), head_at(0, 2), head_at(0, 3), head_at(1, 0)]
+    peers += [head_at(0, 1), head_at(0, 3), head_at(1, 0)]
     for peer in peers:
         pl.semaphore_signal(barrier, inc=1, device_id=peer, device_id_type=MESH)
 
@@ -110,7 +104,10 @@
             continue
         back = next(k for k, at_ in OWNER.items() if at_ == ((NY - dy) % NY, dx))
         gathers[step] = remote(qt.at[A0], qt.at[step], ag_send, ag_recv.at[step], at((NY - dy) % NY, dx))
-        returns[step] = remote(res.at[step], ra.at[back], rs_send, rs_recv, at(dy, dx))
+        returns[step] = [
+            remote(res.at[step], ra.at[back], rs_send, rs_recv, at(dy, dx)),
+            remote(tot.at[step], tot_ra.at[back], tot_send, tot_recv, at(dy, dx)),
+        ]
     pl.semaphore_signal(far_sem, inc=1, device_id=at(0, 1), device_id_type=MESH)
     for dz in (1, 3):
         pl.semaphore_signal(diag_sem, inc=1, device_id=head_at(0, dz), device_id_type=MESH)
@@ -195,10 +192,10 @@
             if c + 1 < HOT_CAP:
                 logits = scores(c + 1)
         if step is not None:
-            res[step, pl.ds(hd, 16), :] = split_sum(jnp.sum(sums, axis=0, keepdims=True), rows)
+            tot[step] = jnp.sum(sums, axis=0, keepdims=True)
         if previous is not None:
             for h in range(kvh):
-                res[previous, pl.ds(0, hd), pl.ds(h * half, half)] = parts[h].astype(BF16)
+                res[previous, :, pl.ds(h * half, half)] = parts[h].astype(BF16)
 
     def page_of(place):
         return jnp.maximum(up_s[0, seq_at(place)] - HOT_CAP, 0)
@@ -268,7 +265,8 @@
         for k in steps:
             @pl.when(step == k)
             def _():
-                returns[k].start()
+                for copy in returns[k]:
+                    copy.start()
 
     def two_steps(n, carry):
         step = 2 * n + 1
@@ -286,7 +284,8 @@
     transpose_values(HOT_CAP)
     lax.fori_loop(0, 3, two_steps, 0)
     shared_block(None, 1, 6)
-    returns[6].start()
+    for copy in returns[6]:
+        copy.start()
     shared_block(7, 1, None)
     shared_block(None, 0, 7)
     own_scores(seqs // 32, seqs // 16)
@@ -298,11 +297,12 @@
 
     own_num = [own_o[pl.ds(h * half, half), pl.ds(h * hd, hd)].T for h in range(kvh)]
     settle(ra, rs_recv)
+    settle(tot_ra, tot_recv)
     whole = summed([res.at[A0], *(ra.at[k] for k in returns)])
-    total = jnp.sum(whole[hd:], axis=0, keepdims=True) + own_t[pl.ds(0, 1), :]
+    total = sum((tot_ra[k] for k in returns), tot[A0]) + own_t[pl.ds(0, 1), :]
     for h in range(kvh):
         lanes = slice(h * half, (h + 1) * half)
-        attended = ((whole[:hd, lanes] + own_num[h]) / total[:, lanes]).T.astype(BF16)
+        attended = ((whole[:, lanes] + own_num[h]) / total[:, lanes]).T.astype(BF16)
         for g in range(half // seqs):
             head = h * (half // seqs) + g
             att[:, pl.ds(head * hd, hd)] = attended[g * seqs : (g + 1) * seqs]
@@ -360,6 +360,7 @@
     settle(hk.at[pl.ds(0, 2 * HOT_CAP)], kv_send)
     settle(qt.at[pl.ds(0, len(gathers))], ag_send)
     settle(ra, rs_send)
+    settle(tot_ra, tot_send)
     for n in range(3):
         settle(zt, z_send.at[n])
     settle(zr.at[0], z_send.at[3])
@@ -393,8 +394,10 @@
             vmem((8, rows), F32),
             vmem((2 * HOT_CAP, 128), F32),
             vmem((2, 2 * HOT_CAP * page, rows), BF16),
-            vmem((8, hd + 16, rows), BF16),
-            vmem((7, hd + 16, rows), BF16),
+            vmem((8, hd, rows), BF16),
+            vmem((7, hd, rows), BF16),
+            vmem((8, 1, rows), F32),
+            vmem((7, 1, rows), F32),
             vmem((page, rows), F32),
             vmem((rows, page), F32),
             vmem((rows, kvh * hd), F32),
@@ -412,6 +415,8 @@
             pltpu.SemaphoreType.DMA((2,)),
             pltpu.SemaphoreType.DMA,
             pltpu.SemaphoreType.DMA((7,)),
+            pltpu.SemaphoreType.DMA,
+            pltpu.SemaphoreType.DMA,
             pltpu.SemaphoreType.DMA,
             pltpu.SemaphoreType.DMA,
             pltpu.SemaphoreType.REGULAR,

time: 32.3 us -> 31.9 us (0.988)
  Pallas kernels: 31.5 us -> 31.1 us
    pallas_call x1, Pallas kernels: 31.5 us -> 31.1 us  [layer(): pl.pallas_call(layer_kernel, out_shape=pltpu.VMEM((seqs // 8, width), F32...]
where the time goes in v8:
time: 31.9 us; the launch traced here: 31.8 us
  Pallas kernels  31.1 us (97%)
  other arithmetic  0.66 us (2%)
    pallas_call x1, Pallas kernels, layer(): pl.pallas_call(layer_kernel, out_shape=pltpu.VMEM((seqs // 8, width), F32...  31.1 us
    convert_element_type x1, other arithmetic, per_device(): return (residual.astype(F32) + normed * norm_gain[None, :]).astype(BF16)  0.66 us

profile of v8, /device:TPU:0, one launch (start us, length us, event | category | flops | bytes accessed | tf_op | source)
XLA Modules:
  0.0 31.8 jit_solution(1850456101805983482)
XLA Ops:
  0.0 0.0 copy-start
  0.0 0.0 copy-start.1
  0.0 31.1 %layer.1 = f32[8,4608]{1,0:T(8,128)S(1)} custom-call(bf16[256,128]{1,0:T(8,128)(2,1)} %bitcast.5, bf16[72,2,128,128]{3,2,1,0:T(8,128)(2,1)} %k_hbm.1, bf16[72,2,128,128]{3,2,1,0:T(8,128)(2,1)} %v_hbm.1, s32[1,64]{1,0:T(1,128)} %bitcast.7, s32[8,128]{1,0:T(8,128)} %bitcast.6, s32[1,64]{1,0:T(1,128)} %bitcast.8, s32[1,64]{1,0:T(1,128)} %bitcast.9, ...), custom_call_target="tpu_custom_call" | custom-call | tf_op jit(solution)/shard_map/layer/pallas_call | solution.py:375
  31.2 0.0 copy-done
  31.2 0.0 copy-done.1
  31.2 0.7 %add_convert_fusion = bf16[8,4608]{1,0:T(8,128)(2,1)} fusion(f32[8,4608]{1,0:T(8,128)S(1)} %layer.1, bf16[8,4608]{1,0:T(8,128)(2,1)S(1)} %copy-done, f32[4608]{0:T(1024)S(1)} %copy-done.1), kind=kLoop, calls=%fused_computation | loop fusion | flops 147456 | bytes 313344 | tf_op jit(solution)/shard_map/convert_element_type | solution.py:445
Async XLA Ops:
  0.0 31.2 %copy-start = (bf16[8,4608]{1,0:T(8,128)(2,1)S(1)}, bf16[8,4608]{1,0:T(8,128)(2,1)}, u32[]{:S(2)}) copy-start(bf16[8,4608]{1,0:T(8,128)(2,1)} %param.18) | copy-start | bytes 221188
  0.0 31.2 %copy-start.1 = (f32[4608]{0:T(1024)S(1)}, f32[4608]{0:T(1024)}, u32[]{:S(2)}) copy-start(f32[4608]{0:T(1024)} %param.19) | copy-start | bytes 55300

commit v9 on v8

--- a/solution.py
+++ b/solution.py
@@ -30,7 +30,7 @@
     q_hbm, k_hbm, v_hbm, hot_hbm, used_hbm, up_hbm, len_hbm, w_hbm, out_ref,
     q_v, hot_v, used_v, len_v, up_s, kbuf, vbuf, hk, hv, vt, qt, qbd, urow, lrow, pos,
     wt, res, ra, tot, tot_ra, own_t, own_w, own_o,
-    w_v, att, pz, zt, zj, zr, near_sum,
+    w_v, att, pz, zr, near_sum,
     in_sem, z_send, z_recv, kv_send, kv_recv, ag_send, ag_recv, rs_send, rs_recv, tot_send, tot_recv, far_sem, diag_sem,
 ):
     seqs = len_v.shape[1]
@@ -110,7 +110,7 @@
         ]
     pl.semaphore_signal(far_sem, inc=1, device_id=at(0, 1), device_id_type=MESH)
     for dz in (1, 3):
-        pl.semaphore_signal(diag_sem, inc=1, device_id=head_at(0, dz), device_id_type=MESH)
+        pl.semaphore_signal(diag_sem.at[0], inc=1, device_id=head_at(0, dz), device_id_type=MESH)
     for step in (B0, A3, A1, A2):
         gathers[step].start()
     local[5].wait()
@@ -247,12 +247,12 @@
 
     set_queries(A0)
     own_t[...] = jnp.zeros_like(own_t)
-    local[7].wait()
-    own_scores(0, seqs // 32)
     pl.semaphore_wait(far_sem, 1)
     for step in (B2, B1, B3):
         gathers[step].start()
     kv_copies[1].start()
+    local[7].wait()
+    own_scores(0, seqs // 64)
     kv_copies[0].wait_recv()
 
     def arrive(step, steps):
@@ -288,7 +288,9 @@
         copy.start()
     shared_block(7, 1, None)
     shared_block(None, 0, 7)
-    own_scores(seqs // 32, seqs // 16)
+    pl.semaphore_wait(diag_sem.at[0], 2)
+    pl.semaphore_signal(diag_sem.at[1], inc=1, device_id=head_at(1, 0), device_id_type=MESH)
+    own_scores(seqs // 64, seqs // 16)
     own_weights()
     own_values()
 
@@ -310,48 +312,31 @@
     local[9].wait()
     block = seqs // NZ
     width = w_v.shape[1] // CHUNKS
-    relayed, plain, joined, across = {}, {}, {}, {}
-    order = [k // 2 + (k % 2) * (CHUNKS // 2) for k in range(CHUNKS)]
-    pl.semaphore_wait(diag_sem, 2)
+    pl.semaphore_wait(diag_sem.at[1], 1)
     def piece_of(k):
         return jnp.dot(att[...], w_v[:, pl.ds(k * width, width)], preferred_element_type=F32).astype(BF16)
 
-    piece = piece_of(order[0])
-    for n, k in enumerate(order):
-        via, other = (1, 3) if k < CHUNKS // 2 else (3, 1)
+    piece = piece_of(0)
+    for k in range(CHUNKS):
         cols = pl.ds(k * width, width)
-        later = piece_of(order[n + 1]) if n + 1 < CHUNKS else None
+        later = piece_of(k + 1) if k + 1 < CHUNKS else None
         for i in range(NZ):
             for j in range(2):
                 pz[i, j, :, cols] = piece[i * block + j * 8 : i * block + j * 8 + 8]
         piece = later
-
-        def to_sum(src, dx, dz, n):
-            slot = 4 if dz == 0 else 2 * dx + dz // 2
-            return remote(src, zr.at[slot, :, cols], z_send.at[n], z_recv.at[CHUNKS + k], head_at(dx, dz))
-
-        relayed[k] = remote(pz.at[(z + 2) % NZ, :, :, cols], zt.at[:, :, cols], z_send.at[0], z_recv.at[k], head_at(0, via))
-        plain[k] = [to_sum(pz.at[(z + other) % NZ, (xl + dx) % 2, :, cols], dx, other, 1) for dx in range(2)]
-        joined[k] = [to_sum(zj.at[(xl + dx) % 2, :, cols], dx, via, 2) for dx in range(2)]
-        across[k] = [to_sum(pz.at[z, 1 - xl, :, cols], 1, 0, 3)]
-        relayed[k].start()
-    for k in order:
-        for copy in (*plain[k], *across[k]):
-            copy.start()
-    for k in order:
-        via = 1 if k < CHUNKS // 2 else 3
+        for dz in (2, 1, 3, 0):
+            for dx in range(2):
+                if dz == 0 and dx == 0:
+                    continue
+                src = pz.at[(z + dz) % NZ, (xl + dx) % 2, :, cols]
+                slot = dx * NZ + dz - 1
+                remote(src, zr.at[slot, :, cols], z_send, z_recv.at[k], head_at(dx, dz)).start()
+    square = jnp.zeros((block // 2, 1), F32)
+    for k in range(CHUNKS):
         cols = pl.ds(k * width, width)
-        relayed[k].wait_recv()
-        for j in range(2):
-            zj[j, :, cols] = (pz[(z + via) % NZ, j, :, cols].astype(F32) + zt[j, :, cols].astype(F32)).astype(BF16)
-        for copy in joined[k]:
-            copy.start()
-    square = jnp.zeros((block // 2, 1), F32)
-    for k in order:
-        cols = pl.ds(k * width, width)
-        settle(zr.at[:, :, cols], z_recv.at[CHUNKS + k])
+        settle(zr.at[:, :, cols], z_recv.at[k])
         projected = pz[z, xl, :, cols].astype(F32)
-        for i in range(5):
+        for i in range(2 * NZ - 1):
             projected = projected + zr[i, :, cols].astype(F32)
         near_sum[:, cols] = projected
         square = square + jnp.sum(projected * projected, axis=1, keepdims=True)
@@ -361,9 +346,7 @@
     settle(qt.at[pl.ds(0, len(gathers))], ag_send)
     settle(ra, rs_send)
     settle(tot_ra, tot_send)
-    for n in range(3):
-        settle(zt, z_send.at[n])
-    settle(zr.at[0], z_send.at[3])
+    settle(zr, z_send)
 
 
 def layer(queries, keys, values, hot_pages, hot_used, user_pages, lengths, o_weight):
@@ -404,13 +387,11 @@
             vmem(o_weight.shape, BF16),
             vmem((seqs, heads * hd), BF16),
             vmem((NZ, 2, 8, width), BF16),
-            vmem((2, 8, width), BF16),
-            vmem((2, 8, width), BF16),
-            vmem((5, 8, width), BF16),
+            vmem((2 * NZ - 1, 8, width), BF16),
             vmem((seqs // 8, width), F32),
             pltpu.SemaphoreType.DMA((10,)),
-            pltpu.SemaphoreType.DMA((4,)),
-            pltpu.SemaphoreType.DMA((2 * CHUNKS,)),
+            pltpu.SemaphoreType.DMA,
+            pltpu.SemaphoreType.DMA((CHUNKS,)),
             pltpu.SemaphoreType.DMA,
             pltpu.SemaphoreType.DMA((2,)),
             pltpu.SemaphoreType.DMA,
@@ -420,7 +401,7 @@
             pltpu.SemaphoreType.DMA,
             pltpu.SemaphoreType.DMA,
             pltpu.SemaphoreType.REGULAR,
-            pltpu.SemaphoreType.REGULAR,
+            pltpu.SemaphoreType.REGULAR((2,)),
         ],
         compiler_params=pltpu.CompilerParams(
             collective_id=0, has_side_effects=True, vmem_limit_bytes=64_500_000

time: 31.9 us -> 30.7 us (0.962)
  Pallas kernels: 31.1 us -> 29.7 us
    pallas_call x1, Pallas kernels: 31.1 us -> 29.7 us  [layer(): pl.pallas_call(layer_kernel, out_shape=pltpu.VMEM((seqs // 8, width), F32...]
where the time goes in v9:
time: 30.7 us; the launch traced here: 30.4 us
  Pallas kernels  29.7 us (97%)
  other arithmetic  0.66 us (2%)
    pallas_call x1, Pallas kernels, layer(): pl.pallas_call(layer_kernel, out_shape=pltpu.VMEM((seqs // 8, width), F32...  29.7 us
    convert_element_type x1, other arithmetic, per_device(): return (residual.astype(F32) + normed * norm_gain[None, :]).astype(BF16)  0.66 us

profile of v9, /device:TPU:0, one launch (start us, length us, event | category | flops | bytes accessed | tf_op | source)
XLA Modules:
  0.0 30.4 jit_solution(13046078233994796667)
XLA Ops:
  0.0 0.0 copy-start
  0.0 0.0 copy-start.1
  0.0 29.7 %layer.1 = f32[8,4608]{1,0:T(8,128)S(1)} custom-call(bf16[256,128]{1,0:T(8,128)(2,1)} %bitcast.5, bf16[72,2,128,128]{3,2,1,0:T(8,128)(2,1)} %k_hbm.1, bf16[72,2,128,128]{3,2,1,0:T(8,128)(2,1)} %v_hbm.1, s32[1,64]{1,0:T(1,128)} %bitcast.7, s32[8,128]{1,0:T(8,128)} %bitcast.6, s32[1,64]{1,0:T(1,128)} %bitcast.8, s32[1,64]{1,0:T(1,128)} %bitcast.9, ...), custom_call_target="tpu_custom_call" | custom-call | tf_op jit(solution)/shard_map/layer/pallas_call | solution.py:358
  29.7 0.0 copy-done
  29.7 0.0 copy-done.1
  29.7 0.7 %add_convert_fusion = bf16[8,4608]{1,0:T(8,128)(2,1)} fusion(f32[8,4608]{1,0:T(8,128)S(1)} %layer.1, bf16[8,4608]{1,0:T(8,128)(2,1)S(1)} %copy-done, f32[4608]{0:T(1024)S(1)} %copy-done.1), kind=kLoop, calls=%fused_computation | loop fusion | flops 147456 | bytes 313344 | tf_op jit(solution)/shard_map/convert_element_type | solution.py:426
Async XLA Ops:
  0.0 29.7 %copy-start = (bf16[8,4608]{1,0:T(8,128)(2,1)S(1)}, bf16[8,4608]{1,0:T(8,128)(2,1)}, u32[]{:S(2)}) copy-start(bf16[8,4608]{1,0:T(8,128)(2,1)} %param.18) | copy-start | bytes 221188
  0.0 29.7 %copy-start.1 = (f32[4608]{0:T(1024)S(1)}, f32[4608]{0:T(1024)}, u32[]{:S(2)}) copy-start(f32[4608]{0:T(1024)} %param.19) | copy-start | bytes 55300
